TPU v7x, 256 devices: a whole 4x4x8 slice. The times are simulated.
256 devices in a mesh: job: 4 (over x), zero: 16 (over z, core), cols: 4 (over y).
Axes of the slice: x: 4, y: 4, z: 8, core: 2. Of those that a mesh axis runs over, the one named last changes fastest.
Arguments:
- weight_gate: bfloat16 [8192, 8192], P(('job', 'zero'), 'cols'), parts along dimension 0, may hold values from -0.1875 to 0.1875
- low_gate: bfloat16 [8192, 32], P(('job', 'zero')), parts along dimension 0, may hold values from -0.125 to 0.125
- high_gate: bfloat16 [128, 8192], P('job', 'cols'), parts along dimension 0, may hold values from -1 to 1
- weight_up: bfloat16 [8192, 8192], P(('job', 'zero'), 'cols'), parts along dimension 0, may hold values from -0.1875 to 0.1875
- low_up: bfloat16 [8192, 32], P(('job', 'zero')), parts along dimension 0, may hold values from -0.125 to 0.125
- high_up: bfloat16 [128, 8192], P('job', 'cols'), parts along dimension 0, may hold values from -1 to 1
- norm_train: float32 [8192], P(('job', 'zero', 'cols')), parts along dimension 0, may hold values from 0.25 to 1.75
- norm_step: float32 [8192], P(('job', 'zero', 'cols')), parts along dimension 0, may hold values from -0.3 to 0.3
Outputs:
- serving_gate: bfloat16 [8192, 8192], P('job', 'cols'), parts along dimension 0
- serving_up: bfloat16 [8192, 8192], P('job', 'cols'), parts along dimension 0
- column_gate: float32 [32768], P(('job', 'cols')), parts along dimension 0
- column_up: float32 [32768], P(('job', 'cols')), parts along dimension 0
- serve_norm: bfloat16 [8192], P('job'), parts along dimension 0
There are 4 independent parts, one for each index of `job`. A program takes and returns all parts, laid end to end along the dimension named above; each array names one. Nothing has to cross between parts.
All inputs are finite; a program needn't handle non-finite values. Where the computation divides by a largest or mean magnitude, that divisor is 1e-20 or more.
Results may differ from a plain program's by a relative error of at most 0.001.
Values may be sent and summed in bfloat16 or wider, within the bound.
A program may use at most 128 MiB of HBM per device.

v0:
```python
import jax
import jax.numpy as jnp
from jax import lax
from jax.sharding import PartitionSpec as P

mix_rate = 2.0


def sent_to_all(shard, axis):
    size = lax.axis_size(axis)
    return lax.all_to_all(
        jnp.broadcast_to(shard[None], (size, *shard.shape)), axis, 0, 0, tiled=True
    )


def over_copies(shard, axis):
    return sent_to_all(shard, axis).max(axis=0)


def in_one(arrays, axis):
    ends = [0]
    for a in arrays:
        ends.append(ends[-1] + a.size)
    total = over_copies(jnp.concatenate([a.ravel() for a in arrays]), axis)
    return tuple((total[b:e].reshape(a.shape) for a, b, e in zip(arrays, ends, ends[1:])))


def in_one_piece(arrays, axis, dim, along):
    both = jnp.concatenate(arrays, axis=along)
    out, at, gathered = (lax.all_gather(both, axis, axis=dim, tiled=True), 0, [])
    for a in arrays:
        gathered.append(lax.slice_in_dim(out, at, at + a.shape[along], axis=along))
        at += a.shape[along]
    return tuple(gathered)


def joined_along(parts, dim):
    parts = jnp.moveaxis(parts, 0, dim)
    dims = parts.shape
    return parts.reshape(*dims[:dim], dims[dim] * dims[dim + 1], *dims[dim + 2 :])


def gather_directly(shard, axis, dim):
    parts = sent_to_all(shard, axis)
    return joined_along(parts, dim)


def per_device(weight_gate, low_gate, high_gate, weight_up, low_up, high_up, norm_train, norm_step):
    whole_gate = weight_gate.astype(jnp.float32) + mix_rate * jnp.dot(
        low_gate, high_gate, preferred_element_type=jnp.float32
    )
    whole_up = weight_up.astype(jnp.float32) + mix_rate * jnp.dot(
        low_up, high_up, preferred_element_type=jnp.float32
    )
    column_gate, column_up = in_one(
        (jnp.max(jnp.abs(whole_gate), axis=0), jnp.max(jnp.abs(whole_up), axis=0)), "zero"
    )
    narrow_gate, narrow_up = (
        (whole_gate / column_gate).astype(jnp.bfloat16),
        (whole_up / column_up).astype(jnp.bfloat16),
    )
    serving_gate, serving_up = in_one_piece((narrow_gate, narrow_up), "zero", 0, 1)
    serve_norm = gather_directly((norm_train + norm_step).astype(jnp.bfloat16), ("zero", "cols"), 0)
    return (serving_gate, serving_up, column_gate, column_up, serve_norm)


def solution(mesh):
    in_specs = (
        P(("job", "zero"), "cols"),
        P(("job", "zero"), None),
        P("job", "cols"),
        P(("job", "zero"), "cols"),
        P(("job", "zero"), None),
        P("job", "cols"),
        P(("job", "zero", "cols")),
        P(("job", "zero", "cols")),
    )
    out_specs = (
        P("job", "cols"),
        P("job", "cols"),
        P(("job", "cols")),
        P(("job", "cols")),
        P("job"),
    )
    return jax.shard_map(
        per_device, mesh=mesh, in_specs=in_specs, out_specs=out_specs, check_vma=False
    )
```

profile of v0, /device:TPU:1, one launch (start us, length us, event | category | flops | bytes accessed | tf_op | source)
XLA Modules:
  0.0 145.7 jit_solution(12326694922828552352)
XLA Ops:
  7.2 0.0 copy-start
  7.2 0.0 copy-start.3
  7.2 0.0 copy-start.4
  7.2 0.0 all-gather.2.cloned.1.call-start
  7.2 0.8 copy-done
  8.1 1.4 abs_reduce_fusion.1
  9.5 1.5 %abs_reduce_fusion = (f32[2048]{0:T(1024)S(1)}, f32[128,2048]{1,0:T(8,128)S(1)}) fusion(bf16[128,32]{0,1:T(8,128)(2,1)} %param.12, bf16[32,2048]{1,0:T(8,128)(2,1)} %param.13, bf16[128,2048]{1,0:T(8,128)(2,1)} %param.11), kind=kOutput, calls=%fused_computation.7 | convolution fusion | flops 18085888 | bytes 1720320 | tf_op jit(solution)/shard_map/dot_general | solution.py:52
  11.0 0.2 broadcast_in_dim.4
  11.2 21.3 %all_to_all.12 = f32[16,1,4096]{2,1,0:T(1,128)S(1)} all-to-all(f32[16,1,4096]{2,1,0:T(1,128)S(1)} %broadcast_in_dim.4), channel_id=1, replica_groups=mesh['job'=4,'zero'=16,'cols'=4] {'zero'}, dimensions={0} | all-to-all | bytes 524288 | tf_op jit(solution)/shard_map/all_to_all | solution.py:11
  32.5 0.2 reduce_max.29
  32.7 0.0 copy-start.1
  32.7 0.0 copy-start.2
  32.7 0.2 divide_convert_fusion
  32.9 1.1 pad_maximum_fusion
  34.0 0.0 all-gather.2.cloned.1.call-update
  34.0 0.0 copy-done.3
  34.0 0.0 copy-done.4
  34.1 15.2 %all_to_all.13 = bf16[64,1,32]{2,1,0:T(2,128)(2,1)S(1)} all-to-all(bf16[64,1,32]{2,1,0:T(2,128)(2,1)S(1)} %broadcast_in_dim.5), channel_id=1, replica_groups=mesh['job'=4,'zero'=16,'cols'=4] {'zero','cols'}, dimensions={0} | all-to-all | bytes 8192 | tf_op jit(solution)/shard_map/all_to_all | solution.py:11
  49.2 0.1 reduce.1
  49.3 0.7 reshape.28
  50.0 76.9 %all-gather.2.cloned.1.call-done = bf16[2048,4096]{1,0:T(8,128)(2,1)} async-done(((bf16[128,4096]{1,0:T(8,128)(2,1)}), bf16[2048,4096]{1,0:T(8,128)(2,1)}) %all-gather.2.cloned.1.call-update) | async-done | bytes 16777232 | tf_op jit(solution)/shard_map/all_gather | solution.py:30
  126.9 11.9 %fusion.2 = (bf16[2048,2048]{1,0:T(8,128)(2,1)}, bf16[2048,2048]{1,0:T(8,128)(2,1)}) fusion(bf16[2048,4096]{1,0:T(8,128)(2,1)} %all-gather.2.cloned.1.call-done), kind=kLoop, calls=%fused_computation.11 | loop fusion | bytes 33554432 | tf_op jit(solution)/shard_map/slice | solution.py:32
  138.8 0.0 copy-done.1
  138.8 0.0 copy-done.2
  (4 shorter events, 0.0 us)
Async XLA Ops:
  7.2 0.9 copy-start
  7.2 26.8 %copy-start.3 = (f32[32]{0:T(128)S(1)}, f32[32]{0:T(128)}, u32[]{:S(2)}) copy-start(f32[32]{0:T(128)} %param.14) | copy-start | bytes 388
  7.2 26.8 %copy-start.4 = (f32[32]{0:T(128)S(1)}, f32[32]{0:T(128)}, u32[]{:S(2)}) copy-start(f32[32]{0:T(128)} %param.15) | copy-start | bytes 388
  7.2 119.6 %all-gather.2.cloned.1.call-start = ((), (), s32[]{:S(2)}) async-start(), calls=%async_computation.2 | async-start | bytes 17825792 | tf_op jit(solution)/shard_map/all_gather | solution.py:30
  32.7 106.1 %copy-start.1 = (f32[2048]{0:T(1024)}, f32[2048]{0:T(1024)S(1)}, u32[]{:S(2)}) copy-start(f32[2048]{0:T(1024)S(1)} %get-tuple-element.7) | copy-start | bytes 24580
  32.7 106.1 %copy-start.2 = (f32[2048]{0:T(1024)}, f32[2048]{0:T(1024)S(1)}, u32[]{:S(2)}) copy-start(f32[2048]{0:T(1024)S(1)} %get-tuple-element.8) | copy-start | bytes 24580
Sparse Core Ops, SparseCore 0:
  34.1 92.6 all-gather.1
where the time goes:
time: 146 us
  waiting for transfers between devices  76.9 us (53%)
  blocking collectives  36.5 us (25%)
  between operations  14.2 us (10%)
  local copies, waits for them, and re-layouts  13.7 us (9%)
  matrix products  2.85 us (2%)
  other arithmetic  1.53 us (1%)
    all_gather x1, waiting for transfers between devices, in_one_piece(): lax.all_gather(both, axis, axis=dim, tiled=True)  76.9 us
    all_to_all x2, blocking collectives, sent_to_all(): lax.all_to_all(jnp.broadcast_to(shard[None], (size, *shard.shape)), axis,...  36.5 us
    slice x1, local copies, waits for them, and re-layouts, in_one_piece(): gathered.append(lax.slice_in_dim(out, at, at + a.shape[along], axis=along))  11.9 us
  transfers between devices with their start and end apart: 1, of which 1 were waited for; matrix products, arithmetic and copies ran while one was open for 1% of the time, Pallas kernels for 0%

commit v1 on v0

v1 whole, which is shorter than its diff:
```python
import functools

import jax
import jax.numpy as jnp
from jax import lax
from jax.experimental import pallas as pl
from jax.experimental.pallas import tpu as pltpu
from jax.sharding import PartitionSpec as P

mix_rate = 2.0
MESH = pl.DeviceIdType.MESH
CH = 4
TILE = 512
LANES = 128


def remote(src, dst, send_sem, recv_sem, device_id):
    return pltpu.make_async_remote_copy(
        src_ref=src, dst_ref=dst, send_sem=send_sem, recv_sem=recv_sem, device_id=device_id, device_id_type=MESH
    )


def kernel(
    nz, ny,
    wg_hbm, lg_hbm, hg_hbm, wu_hbm, lu_hbm, hu_hbm, nt_hbm, ns_hbm,
    og, ou, col_out, norm_out,
    w_in, l_in, h_in, n_in, whole, pmax, pget, cmax, allmax, ybuf, zbuf,
    in_sem, ring_send, ring_recv, pair_send, pair_recv, max_send, max_recv, ny_send, ny_recv, nz_send, nz_recv,
):
    zero, col = lax.axis_index("zero"), lax.axis_index("cols")
    z, core = zero // 2, zero % 2
    outs = (og, ou)
    rows, columns = w_in.shape[1:]
    step_rows = rows // CH

    loads = [
        pltpu.make_async_copy(src, dst, in_sem.at[i])
        for i, (src, dst) in enumerate(
            (
                (lg_hbm, l_in.at[0]), (hg_hbm, h_in.at[0]), (wg_hbm, w_in.at[0]),
                (lu_hbm, l_in.at[1]), (hu_hbm, h_in.at[1]), (wu_hbm, w_in.at[1]),
                (nt_hbm, n_in.at[0]), (ns_hbm, n_in.at[1]),
            )
        )
    ]
    for c in loads:
        c.start()

    barrier = pltpu.get_barrier_semaphore()
    peer = zero + 1 - 2 * core
    others = [(z + d) % nz * 2 + core for d in range(1, nz)]
    others_cross = [(z + d) % nz * 2 + 1 - core for d in range(1, nz)]
    for t in others + others_cross + [peer]:
        pl.semaphore_signal(barrier, 1, device_id={"zero": t}, device_id_type=MESH)
    for d in range(1, ny):
        pl.semaphore_signal(barrier, 1, device_id={"cols": (col + d) % ny}, device_id_type=MESH)

    for m in range(2):
        for i in range(3):
            loads[3 * m + i].wait()
        for t in range(columns // TILE):
            at = slice(t * TILE, (t + 1) * TILE)
            new = w_in[m, :, at].astype(jnp.float32) + mix_rate * lax.dot_general(
                l_in[m], h_in[m, :, at], (((0,), (0,)), ((), ())), preferred_element_type=jnp.float32
            )
            whole[m, :, at] = new
            top = jnp.max(jnp.abs(new), axis=0, keepdims=True)
            for q in range(TILE // LANES):
                r = t * (TILE // LANES) + q
                pmax[m, r : r + 1, :] = top[:, q * LANES : (q + 1) * LANES]
    loads[6].wait()
    loads[7].wait()
    gain = n_in[0] + n_in[1]
    ybuf[pl.ds(col, 1)] = jnp.concatenate([gain] * ny, axis=1)[None]

    pl.semaphore_wait(barrier, 2 * nz - 1 + ny - 1)

    first = remote(pmax.at[1 - core], pget, max_send.at[0], max_recv.at[0], {"zero": peer})
    first.start()
    norm_y = [
        remote(ybuf.at[col], ybuf.at[col], ny_send.at[d - 1], ny_recv.at[d - 1], {"cols": (col + d) % ny})
        for d in range(1, ny)
    ]
    for c in norm_y:
        c.start()
    first.wait_recv()
    cmax[...] = jnp.maximum(pmax[core], pget[...])
    spread = [
        remote(cmax, allmax.at[d], max_send.at[d], max_recv.at[d], {"zero": others[d - 1]}) for d in range(1, nz)
    ]
    for c in spread:
        c.start()
    for c in norm_y:
        c.wait_recv()
    lane = lax.broadcasted_iota(jnp.int32, (1, LANES), 1) // (LANES // ny)
    row = ybuf[0]
    for k in range(1, ny):
        row = jnp.where(lane == k, ybuf[k], row)
    zbuf[pl.ds(zero, 1)] = row[None]
    top = cmax[...]
    for d, c in enumerate(spread):
        c.wait_recv()
        top = jnp.maximum(top, allmax[d + 1])
    col_out[pl.ds(core, 1)] = top[None]
    back = remote(col_out.at[core], col_out.at[core], max_send.at[nz], max_recv.at[nz], {"zero": peer})
    back.start()
    norm_z = [
        remote(zbuf.at[zero], zbuf.at[zero], nz_send.at[i], nz_recv.at[i], {"zero": t})
        for i, t in enumerate(others + others_cross + [peer])
    ]
    for c in norm_z:
        c.start()
    back.wait_recv()

    mine = pl.multiple_of(zero * rows, rows)
    for m in range(2):
        for r in range(columns // LANES):
            at = slice(r * LANES, (r + 1) * LANES)
            inv = 1.0 / col_out[m, r : r + 1, :]
            outs[m][pl.ds(mine, rows), at] = (whole[m, :, at] * inv).astype(jnp.bfloat16)

    to = ((z + 1) % nz * 2 + core, (z + nz - 1) % nz * 2 + core)
    half = nz // 2

    def piece(d, s, k):
        b = (z - s + nz) % nz if d == 0 else (z + s) % nz
        m = k // CH if d == 0 else 1 - k // CH
        at = pl.multiple_of((b * 2 + core) * rows + k % CH * step_rows, step_rows)
        return m, outs[m].at[pl.ds(at, step_rows)]

    def ring(d, s, k):
        _, ref = piece(d, s, k)
        return remote(ref, ref, ring_send.at[d], ring_recv.at[d, s, k], {"zero": to[d]})

    def pair(d, s, k):
        m, ref = piece(d, s, k)
        slot = s if d == m else (nz - s) % nz
        return remote(ref, ref, pair_send, pair_recv.at[m, slot], {"zero": peer})

    for k in range(2 * CH):
        for d in range(2):
            ring(d, 0, k).start()
    for k in range(2 * CH):
        pair(0, 0, k).start()
    for s in range(1, half + 1):
        for k in range(2 * CH if s < half else CH):
            for d in range(2):
                ring(d, s - 1, k).wait_recv()
                if s < half - 1 or s == half - 1 and k < CH:
                    ring(d, s, k).start()
                pair(d, s, k).start()

    for c in norm_z:
        c.wait_recv()
    norm_out[...] = zbuf[:, 0, :]
    for m in range(2):
        for slot in range(nz):
            block = outs[m].at[pl.ds(0, rows)]
            remote(block, block, pair_send, pair_recv.at[m, slot], {"zero": peer}).wait_recv()
    total = og.at[pl.ds(0, rows * (nz - 1))]
    for d in range(2):
        remote(total, total, ring_send.at[d], ring_recv.at[d, 0, 0], {"zero": to[d]}).wait_send()
    remote(og, og, pair_send, pair_recv.at[0, 0], {"zero": peer}).wait_send()
    for c in [first, *norm_y, *spread, back, *norm_z]:
        c.wait_send()


def per_device(weight_gate, low_gate, high_gate, weight_up, low_up, high_up, norm_train, norm_step):
    devices, ny = lax.axis_size("zero"), lax.axis_size("cols")
    nz = devices // 2
    rows, columns = weight_gate.shape
    rank = low_gate.shape[1]
    share = norm_train.shape[0]
    tiles = columns // LANES
    f32, bf16 = jnp.float32, jnp.bfloat16
    hbm = pl.BlockSpec(memory_space=pltpu.HBM)
    vmem = pl.BlockSpec(memory_space=pltpu.VMEM)
    dma = pltpu.SemaphoreType.DMA
    serving_gate, serving_up, column, norm = pl.pallas_call(
        functools.partial(kernel, nz, ny),
        out_shape=(
            pltpu.VMEM((devices * rows, columns), bf16),
            pltpu.VMEM((devices * rows, columns), bf16),
            pltpu.VMEM((2, tiles, LANES), f32),
            pltpu.VMEM((devices, LANES), f32),
        ),
        in_specs=[hbm] * 8,
        out_specs=(vmem,) * 4,
        scratch_shapes=[
            pltpu.VMEM((2, rows, columns), bf16),
            pltpu.VMEM((2, rank, rows), bf16),
            pltpu.VMEM((2, rank, columns), bf16),
            pltpu.VMEM((2, 1, share), f32),
            pltpu.VMEM((2, rows, columns), f32),
            pltpu.VMEM((2, tiles, LANES), f32),
            pltpu.VMEM((tiles, LANES), f32),
            pltpu.VMEM((tiles, LANES), f32),
            pltpu.VMEM((nz, tiles, LANES), f32),
            pltpu.VMEM((ny, 1, LANES), f32),
            pltpu.VMEM((devices, 1, LANES), f32),
            dma((8,)),
            dma((2,)),
            dma((2, nz // 2, 2 * CH)),
            dma,
            dma((2, nz)),
            dma((nz + 1,)),
            dma((nz + 1,)),
            dma((max(ny - 1, 1),)),
            dma((max(ny - 1, 1),)),
            dma((devices - 1,)),
            dma((devices - 1,)),
        ],
        compiler_params=pltpu.CompilerParams(
            collective_id=0, has_side_effects=True, vmem_limit_bytes=47 << 20
        ),
    )(
        weight_gate, low_gate.T, high_gate, weight_up, low_up.T, high_up,
        norm_train.reshape(1, share), norm_step.reshape(1, share),
    )
    column = column.reshape(2, columns)
    return (serving_gate, serving_up, column[0], column[1], norm.reshape(-1).astype(bf16))


def solution(mesh):
    in_specs = (
        P(("job", "zero"), "cols"),
        P(("job", "zero"), None),
        P("job", "cols"),
        P(("job", "zero"), "cols"),
        P(("job", "zero"), None),
        P("job", "cols"),
        P(("job", "zero", "cols")),
        P(("job", "zero", "cols")),
    )
    out_specs = (
        P("job", "cols"),
        P("job", "cols"),
        P(("job", "cols")),
        P(("job", "cols")),
        P("job"),
    )
    return jax.shard_map(
        per_device, mesh=mesh, in_specs=in_specs, out_specs=out_specs, check_vma=False
    )
```

time: 146 us -> 108 us (0.74)
  Pallas kernels: 0 us -> 98.8 us
  waiting for transfers between devices: 76.9 us -> 0 us
  blocking collectives: 36.5 us -> 0 us
  between operations: 14.2 us -> 0.64 us
  local copies, waits for them, and re-layouts: 13.7 us -> 7.4 us
  matrix products: 2.85 us -> 0 us
    pallas_call x0 -> x1, Pallas kernels: none -> 98.8 us  [per_device(): pl.pallas_call(functools.partial(kernel, nz, ny), out_shape=(pltpu.VMEM((...]
    all_gather x1 -> x0, waiting for transfers between devices: 76.9 us -> none  [in_one_piece(): lax.all_gather(both, axis, axis=dim, tiled=True)]
    all_to_all x2 -> x0, blocking collectives: 36.5 us -> none  [sent_to_all(): lax.all_to_all(jnp.broadcast_to(shard[None], (size, *shard.shape)), axis,...]
    slice x2 -> x0, local copies, waits for them, and re-layouts: 12 us -> none  [the longest x1 11.9 us: in_one_piece(): gathered.append(lax.slice_in_dim(out, at, at + a.shape[along], axis=along))]
    unnamed x10 -> x2, local copies, waits for them, and re-layouts: 0.86 us -> 6.8 us
    dot_general x2 -> x0, matrix products: 2.85 us -> none  [the longest x1 1.46 us: per_device(): jnp.dot(low_up, high_up, preferred_element_type=jnp.float32)]
  transfers between devices with their start and end apart: 1 -> 0, of which waited for: 1 -> 0; matrix products, arithmetic and copies ran while one was open for 1% -> 0% of each run, Pallas kernels for 0% -> 0%
where the time goes in v1:
time: 108 us; the launch traced here: 107 us
  Pallas kernels  98.8 us (91%)
  local copies, waits for them, and re-layouts  7.4 us (7%)
    pallas_call x1, Pallas kernels, per_device(): pl.pallas_call(functools.partial(kernel, nz, ny), out_shape=(pltpu.VMEM((...  98.8 us
    unnamed x2, local copies, waits for them, and re-layouts  6.8 us

profile of v1, /device:TPU:1, one launch (start us, length us, event | category | flops | bytes accessed | tf_op | source)
XLA Modules:
  0.0 107.5 jit_solution(10599082940894845766)
XLA Ops:
  0.6 98.8 %shard_map.119 = (bf16[2048,2048]{1,0:T(8,128)(2,1)S(1)}, bf16[2048,2048]{1,0:T(8,128)(2,1)S(1)}, f32[2,16,128]{2,1,0:T(8,128)S(1)}, f32[16,128]{1,0:T(8,128)S(1)}) custom-call(bf16[128,2048]{1,0:T(8,128)(2,1)} %wg_hbm.1, bf16[32,128]{1,0:T(8,128)(2,1)} %bitcast.10, bf16[32,2048]{1,0:T(8,128)(2,1)} %hg_hbm.1, bf16[128,2048]{1,0:T(8,128)(2,1)} %wu_hbm.1, ...), custom_call_target="tpu_custom_call" | custom-call | tf_op jit(solution)/shard_map/pallas_call | solution.py:179
  99.5 3.4 %copy.15 = bf16[2048,2048]{1,0:T(8,128)(2,1)} copy(bf16[2048,2048]{1,0:T(8,128)(2,1)S(1)} %get-tuple-element.15) | data formatting | bytes 16777216
  102.9 0.6 convert_bitcast_fusion
  103.5 0.6 slice_bitcast_fusion
  104.1 3.4 %copy.16 = bf16[2048,2048]{1,0:T(8,128)(2,1)} copy(bf16[2048,2048]{1,0:T(8,128)(2,1)S(1)} %get-tuple-element.16) | data formatting | bytes 16777216

commit v2 on v1

--- a/solution.py
+++ b/solution.py
@@ -11,6 +11,7 @@
 MESH = pl.DeviceIdType.MESH
 CH = 4
 TILE = 512
+DEPTH = 4
 LANES = 128
 
 
@@ -24,14 +25,17 @@
     nz, ny,
     wg_hbm, lg_hbm, hg_hbm, wu_hbm, lu_hbm, hu_hbm, nt_hbm, ns_hbm,
     og, ou, col_out, norm_out,
-    w_in, l_in, h_in, n_in, whole, pmax, pget, cmax, allmax, ybuf, zbuf,
-    in_sem, ring_send, ring_recv, pair_send, pair_recv, max_send, max_recv, ny_send, ny_recv, nz_send, nz_recv,
+    w_in, l_in, h_in, n_in, raw, l_raw, whole, pmax, pget, cmax, allmax, inv, ybuf, zbuf,
+    in_sem, ring_send, ring_recv, low_send, low_recv, pair_send, pair_recv,
+    max_send, max_recv, ny_send, ny_recv, nz_send, nz_recv,
 ):
     zero, col = lax.axis_index("zero"), lax.axis_index("cols")
     z, core = zero // 2, zero % 2
     outs = (og, ou)
     rows, columns = w_in.shape[1:]
     step_rows = rows // CH
+    half = nz // 2
+    pieces = (2 * half - 1) * CH
 
     loads = [
         pltpu.make_async_copy(src, dst, in_sem.at[i])
@@ -55,14 +59,17 @@
     for d in range(1, ny):
         pl.semaphore_signal(barrier, 1, device_id={"cols": (col + d) % ny}, device_id_type=MESH)
 
+    def merged(weights, low, m, at):
+        return weights[:, at].astype(jnp.float32) + mix_rate * lax.dot_general(
+            low[...], h_in[m, :, at], (((0,), (0,)), ((), ())), preferred_element_type=jnp.float32
+        )
+
     for m in range(2):
         for i in range(3):
             loads[3 * m + i].wait()
         for t in range(columns // TILE):
             at = slice(t * TILE, (t + 1) * TILE)
-            new = w_in[m, :, at].astype(jnp.float32) + mix_rate * lax.dot_general(
-                l_in[m], h_in[m, :, at], (((0,), (0,)), ((), ())), preferred_element_type=jnp.float32
-            )
+            new = merged(w_in.at[m], l_in.at[m], m, at)
             whole[m, :, at] = new
             top = jnp.max(jnp.abs(new), axis=0, keepdims=True)
             for q in range(TILE // LANES):
@@ -73,6 +80,36 @@
     gain = n_in[0] + n_in[1]
     ybuf[pl.ds(col, 1)] = jnp.concatenate([gain] * ny, axis=1)[None]
 
+    to = ((z + 1) % nz * 2 + core, (z + nz - 1) % nz * 2 + core)
+
+    def block_rows(d, s):
+        b = (z - s + nz) % nz if d == 0 else (z + s) % nz
+        return (b * 2 + core) * rows
+
+    def piece(d, i, hops):
+        k = i % (2 * CH)
+        m = k // CH if d == 0 else 1 - k // CH
+        at = pl.multiple_of(block_rows(d, i // (2 * CH) + hops) + k % CH * step_rows, step_rows)
+        return m, outs[m].at[pl.ds(at, step_rows)]
+
+    def ring(d, i):
+        if i < CH:
+            at = pl.ds(i * step_rows, step_rows)
+            src, dst = w_in.at[d, at], raw.at[d, at]
+        else:
+            _, src = piece(d, i, 0)
+            dst = src
+        return remote(src, dst, ring_send.at[d, i % DEPTH], ring_recv.at[d, i], {"zero": to[d]})
+
+    def pair(d, i):
+        m, ref = piece(d, i, 1)
+        s = i // (2 * CH) + 1
+        slot = s if d == m else (nz - s) % nz
+        return remote(ref, ref, pair_send, pair_recv.at[m, slot], {"zero": peer})
+
+    def low(d):
+        return remote(l_in.at[d], l_raw.at[d], low_send.at[d], low_recv.at[d], {"zero": to[d]})
+
     pl.semaphore_wait(barrier, 2 * nz - 1 + ny - 1)
 
     first = remote(pmax.at[1 - core], pget, max_send.at[0], max_recv.at[0], {"zero": peer})
@@ -83,6 +120,9 @@
     ]
     for c in norm_y:
         c.start()
+    for d in range(2):
+        low(d).start()
+        ring(d, 0).start()
     first.wait_recv()
     cmax[...] = jnp.maximum(pmax[core], pget[...])
     spread = [
@@ -90,6 +130,9 @@
     ]
     for c in spread:
         c.start()
+    for i in range(1, min(DEPTH, CH)):
+        for d in range(2):
+            ring(d, i).start()
     for c in norm_y:
         c.wait_recv()
     lane = lax.broadcasted_iota(jnp.int32, (1, LANES), 1) // (LANES // ny)
@@ -111,44 +154,51 @@
     for c in norm_z:
         c.start()
     back.wait_recv()
+    for m in range(2):
+        for r in range(columns // LANES):
+            inv[m, :, r * LANES : (r + 1) * LANES] = 1.0 / col_out[m, r : r + 1, :]
 
     mine = pl.multiple_of(zero * rows, rows)
     for m in range(2):
-        for r in range(columns // LANES):
-            at = slice(r * LANES, (r + 1) * LANES)
-            inv = 1.0 / col_out[m, r : r + 1, :]
-            outs[m][pl.ds(mine, rows), at] = (whole[m, :, at] * inv).astype(jnp.bfloat16)
-
-    to = ((z + 1) % nz * 2 + core, (z + nz - 1) % nz * 2 + core)
-    half = nz // 2
-
-    def piece(d, s, k):
-        b = (z - s + nz) % nz if d == 0 else (z + s) % nz
-        m = k // CH if d == 0 else 1 - k // CH
-        at = pl.multiple_of((b * 2 + core) * rows + k % CH * step_rows, step_rows)
-        return m, outs[m].at[pl.ds(at, step_rows)]
-
-    def ring(d, s, k):
-        _, ref = piece(d, s, k)
-        return remote(ref, ref, ring_send.at[d], ring_recv.at[d, s, k], {"zero": to[d]})
-
-    def pair(d, s, k):
-        m, ref = piece(d, s, k)
-        slot = s if d == m else (nz - s) % nz
-        return remote(ref, ref, pair_send, pair_recv.at[m, slot], {"zero": peer})
-
-    for k in range(2 * CH):
+        for t in range(columns // TILE):
+            at = slice(t * TILE, (t + 1) * TILE)
+            outs[m][pl.ds(mine, rows), at] = (whole[m, :, at] * inv[m, :, at]).astype(jnp.bfloat16)
+
+    def send(d, i):
+        if i >= DEPTH:
+            ring(d, i - DEPTH).wait_send()
+        ring(d, i).start()
+
+    def receive(d, i):
+        ring(d, i).wait_recv()
+        pair(d, i).start()
+
+    for i in range(min(DEPTH, CH), pieces):
+        if i == CH:
+            for m in range(2):
+                block = outs[m].at[pl.ds(mine, rows)]
+                remote(block, block, pair_send, pair_recv.at[m, 0], {"zero": peer}).start()
+        if i == 2 * CH:
+            for d in range(2):
+                low(d).wait_recv()
+                for k in range(CH):
+                    ring(d, k).wait_recv()
+                near = pl.multiple_of(block_rows(d, 1), rows)
+                for t in range(columns // TILE):
+                    at = slice(t * TILE, (t + 1) * TILE)
+                    new = merged(raw.at[d], l_raw.at[d], d, at) * inv[d, :, at]
+                    outs[d][pl.ds(near, rows), at] = new.astype(jnp.bfloat16)
+            for d in range(2):
+                for k in range(CH):
+                    pair(d, k).start()
         for d in range(2):
-            ring(d, 0, k).start()
-    for k in range(2 * CH):
-        pair(0, 0, k).start()
-    for s in range(1, half + 1):
-        for k in range(2 * CH if s < half else CH):
+            send(d, i)
+        if i >= CH + DEPTH:
             for d in range(2):
-                ring(d, s - 1, k).wait_recv()
-                if s < half - 1 or s == half - 1 and k < CH:
-                    ring(d, s, k).start()
-                pair(d, s, k).start()
+                receive(d, i - DEPTH)
+    for i in range(pieces - DEPTH, pieces):
+        for d in range(2):
+            receive(d, i)
 
     for c in norm_z:
         c.wait_recv()
@@ -157,12 +207,33 @@
         for slot in range(nz):
             block = outs[m].at[pl.ds(0, rows)]
             remote(block, block, pair_send, pair_recv.at[m, slot], {"zero": peer}).wait_recv()
-    total = og.at[pl.ds(0, rows * (nz - 1))]
     for d in range(2):
-        remote(total, total, ring_send.at[d], ring_recv.at[d, 0, 0], {"zero": to[d]}).wait_send()
+        low(d).wait_send()
+        for i in range(pieces - DEPTH, pieces):
+            ring(d, i).wait_send()
     remote(og, og, pair_send, pair_recv.at[0, 0], {"zero": peer}).wait_send()
     for c in [first, *norm_y, *spread, back, *norm_z]:
         c.wait_send()
+
+
+def write_out(parts, *refs):
+    ins, outs, (scratch, sem) = refs[:4], refs[4:9], refs[9:]
+    size = ins[0].shape[0] // parts
+    copies = [
+        pltpu.make_async_copy(
+            ins[m].at[pl.ds(i * size, size)], outs[m].at[pl.ds(i * size, size)], sem.at[m * parts + i]
+        )
+        for i in range(parts)
+        for m in range(2)
+    ]
+    copies += [pltpu.make_async_copy(ins[2].at[m], outs[2 + m], sem.at[2 * parts + m]) for m in range(2)]
+    for c in copies:
+        c.start()
+    scratch[...] = ins[3][...].astype(jnp.bfloat16)
+    last = pltpu.make_async_copy(scratch, outs[4], sem.at[2 * parts + 2])
+    last.start()
+    for c in copies + [last]:
+        c.wait()
 
 
 def per_device(weight_gate, low_gate, high_gate, weight_up, low_up, high_up, norm_train, norm_step):
@@ -191,16 +262,21 @@
             pltpu.VMEM((2, rank, rows), bf16),
             pltpu.VMEM((2, rank, columns), bf16),
             pltpu.VMEM((2, 1, share), f32),
+            pltpu.VMEM((2, rows, columns), bf16),
+            pltpu.VMEM((2, rank, rows), bf16),
             pltpu.VMEM((2, rows, columns), f32),
             pltpu.VMEM((2, tiles, LANES), f32),
             pltpu.VMEM((tiles, LANES), f32),
             pltpu.VMEM((tiles, LANES), f32),
             pltpu.VMEM((nz, tiles, LANES), f32),
+            pltpu.VMEM((2, 1, columns), f32),
             pltpu.VMEM((ny, 1, LANES), f32),
             pltpu.VMEM((devices, 1, LANES), f32),
             dma((8,)),
+            dma((2, DEPTH)),
+            dma((2, (nz - 1) * CH)),
             dma((2,)),
-            dma((2, nz // 2, 2 * CH)),
+            dma((2,)),
             dma,
             dma((2, nz)),
             dma((nz + 1,)),
@@ -217,8 +293,22 @@
         weight_gate, low_gate.T, high_gate, weight_up, low_up.T, high_up,
         norm_train.reshape(1, share), norm_step.reshape(1, share),
     )
-    column = column.reshape(2, columns)
-    return (serving_gate, serving_up, column[0], column[1], norm.reshape(-1).astype(bf16))
+    parts = 4
+    serving_gate, serving_up, column_gate, column_up, norm = pl.pallas_call(
+        functools.partial(write_out, parts),
+        out_shape=(
+            jax.ShapeDtypeStruct((devices * rows, columns), bf16),
+            jax.ShapeDtypeStruct((devices * rows, columns), bf16),
+            jax.ShapeDtypeStruct((tiles, LANES), f32),
+            jax.ShapeDtypeStruct((tiles, LANES), f32),
+            jax.ShapeDtypeStruct((devices, LANES), bf16),
+        ),
+        in_specs=[vmem] * 4,
+        out_specs=(hbm,) * 5,
+        scratch_shapes=[pltpu.VMEM((devices, LANES), bf16), dma((2 * parts + 3,))],
+        compiler_params=pltpu.CompilerParams(vmem_limit_bytes=20 << 20),
+    )(serving_gate, serving_up, column, norm)
+    return (serving_gate, serving_up, column_gate.reshape(-1), column_up.reshape(-1), norm.reshape(-1))
 
 
 def solution(mesh):

time: 108 us -> 101 us (0.935)
  local copies, waits for them, and re-layouts: 7.4 us -> 0 us
  Pallas kernels: 98.8 us -> 100 us
    unnamed x2 -> x0, local copies, waits for them, and re-layouts: 6.8 us -> none
    pallas_call x0 -> x1, Pallas kernels: none -> 5.96 us  [per_device(): pl.pallas_call(functools.partial(write_out, parts), out_shape=(jax.ShapeD...]
    pallas_call x1, Pallas kernels: 98.8 us -> 94.1 us  [per_device(): pl.pallas_call(functools.partial(kernel, nz, ny), out_shape=(pltpu.VMEM((...]
where the time goes in v2:
time: 101 us
  Pallas kernels  100 us (99%)
    pallas_call x1, Pallas kernels, per_device(): pl.pallas_call(functools.partial(kernel, nz, ny), out_shape=(pltpu.VMEM((...  94.1 us
    pallas_call x1, Pallas kernels, per_device(): pl.pallas_call(functools.partial(write_out, parts), out_shape=(jax.ShapeD...  5.96 us

profile of v2, /device:TPU:1, one launch (start us, length us, event | category | flops | bytes accessed | tf_op | source)
XLA Modules:
  0.0 100.7 jit_solution(5924921522474685220)
XLA Ops:
  0.6 94.1 %shard_map.119 = (bf16[2048,2048]{1,0:T(8,128)(2,1)S(1)}, bf16[2048,2048]{1,0:T(8,128)(2,1)S(1)}, f32[2,16,128]{2,1,0:T(8,128)S(1)}, f32[16,128]{1,0:T(8,128)S(1)}) custom-call(bf16[128,2048]{1,0:T(8,128)(2,1)} %wg_hbm.1, bf16[32,128]{1,0:T(8,128)(2,1)} %bitcast.7, bf16[32,2048]{1,0:T(8,128)(2,1)} %hg_hbm.1, bf16[128,2048]{1,0:T(8,128)(2,1)} %wu_hbm.1, ...), custom_call_target="tpu_custom_call" | custom-call | tf_op jit(solution)/shard_map/pallas_call | solution.py:250
  94.7 6.0 %shard_map.120 = (bf16[2048,2048]{1,0:T(8,128)(2,1)}, bf16[2048,2048]{1,0:T(8,128)(2,1)}, f32[16,128]{1,0:T(8,128)}, f32[16,128]{1,0:T(8,128)}, bf16[16,128]{1,0:T(8,128)(2,1)}) custom-call(bf16[2048,2048]{1,0:T(8,128)(2,1)S(1)} %get-tuple-element.14.refs_0_, bf16[2048,2048]{1,0:T(8,128)(2,1)S(1)} %get-tuple-element.15.refs_1_, ...), custom_call_target="tpu_custom_call" | custom-call | tf_op jit(solution)/shard_map/pallas_call | solution.py:297

commit v3 on v2

v3 whole, which is shorter than its diff:
```python
import functools

import jax
import jax.numpy as jnp
from jax import lax
from jax.experimental import pallas as pl
from jax.experimental.pallas import tpu as pltpu
from jax.sharding import PartitionSpec as P

mix_rate = 2.0
MESH = pl.DeviceIdType.MESH
CH = 4
TILE = 512
DEPTH = 8
LAG = 6
EARLY = 3
LANES = 128


def remote(src, dst, send_sem, recv_sem, device_id):
    return pltpu.make_async_remote_copy(
        src_ref=src, dst_ref=dst, send_sem=send_sem, recv_sem=recv_sem, device_id=device_id, device_id_type=MESH
    )


def kernel(
    nz, ny,
    wg_hbm, lg_hbm, hg_hbm, wu_hbm, lu_hbm, hu_hbm, nt_hbm, ns_hbm,
    og, ou, col_out, norm_out,
    w_in, l_in, h_in, n_in, raw, l_raw, whole, pmax, pget, cmax, allmax, inv, ybuf, zbuf,
    in_sem, ring_send, ring_recv, low_send, low_recv, pair_send, pair_recv,
    max_send, max_recv, ny_send, ny_recv, nz_send, nz_recv, known,
):
    zero, col = lax.axis_index("zero"), lax.axis_index("cols")
    z, core = zero // 2, zero % 2
    outs = (og, ou)
    rows, columns = w_in.shape[1:]
    step_rows = rows // CH
    half = nz // 2
    own = 2 * CH
    pieces = (2 * half - 1) * CH

    loads = [
        pltpu.make_async_copy(src, dst, in_sem.at[i])
        for i, (src, dst) in enumerate(
            (
                (wg_hbm, w_in.at[0]), (wu_hbm, w_in.at[1]), (lg_hbm, l_in.at[0]), (lu_hbm, l_in.at[1]),
                (hg_hbm, h_in.at[0]), (hu_hbm, h_in.at[1]), (nt_hbm, n_in.at[0]), (ns_hbm, n_in.at[1]),
            )
        )
    ]
    for c in loads:
        c.start()

    barrier = pltpu.get_barrier_semaphore()
    peer = zero + 1 - 2 * core
    to = ((z + 1) % nz * 2 + core, (z + nz - 1) % nz * 2 + core)
    others = [(z + d) % nz * 2 + core for d in range(1, nz)]
    next_col, last_col = (col + 1) % ny, (col + ny - 1) % ny
    for t in (*to, peer):
        pl.semaphore_signal(barrier, 1, device_id={"zero": t}, device_id_type=MESH)
    for t in (next_col, last_col):
        pl.semaphore_signal(barrier, 1, device_id={"cols": t}, device_id_type=MESH)

    def know(hops):
        pl.semaphore_wait(known.at[hops - 2], 2)

    def tell(hops):
        for t in to:
            pl.semaphore_signal(known.at[hops - 2], 1, device_id={"zero": t}, device_id_type=MESH)

    def merged(weights, low, m, at):
        return weights[:, at].astype(jnp.float32) + mix_rate * lax.dot_general(
            low[...], h_in[m, :, at], (((0,), (0,)), ((), ())), preferred_element_type=jnp.float32
        )

    def maxima(m):
        for t in range(columns // TILE):
            at = slice(t * TILE, (t + 1) * TILE)
            new = merged(w_in.at[m], l_in.at[m], m, at)
            whole[m, :, at] = new
            top = jnp.max(jnp.abs(new), axis=0, keepdims=True)
            for q in range(TILE // LANES):
                r = t * (TILE // LANES) + q
                pmax[m, r : r + 1, :] = top[:, q * LANES : (q + 1) * LANES]

    def block_rows(d, s):
        b = (z - s + nz) % nz if d == 0 else (z + s) % nz
        return (b * 2 + core) * rows

    def matrix(d, k):
        return k // CH if d == 0 else 1 - k // CH

    def piece(d, i, hops):
        k = i % own
        at = pl.multiple_of(block_rows(d, i // own + hops) + k % CH * step_rows, step_rows)
        return outs[matrix(d, k)].at[pl.ds(at, step_rows)]

    def ring(d, i):
        if i < own:
            m, at = matrix(d, i), pl.ds(i % CH * step_rows, step_rows)
            src, dst = w_in.at[m, at], raw.at[d, m, at]
        else:
            src = dst = piece(d, i, 0)
        return remote(src, dst, ring_send.at[d, i % DEPTH], ring_recv.at[d, i], {"zero": to[d]})

    def pair(d, i):
        ref = piece(d, i, 1)
        s = i // own + 1
        slot = s if d == matrix(d, i % own) else (nz - s) % nz
        return remote(ref, ref, pair_send, pair_recv.at[matrix(d, i % own), slot], {"zero": peer})

    def low(d):
        return remote(l_in, l_raw.at[d], low_send.at[d], low_recv.at[d], {"zero": to[d]})

    def norm_y(h):
        row = ybuf.at[(col + ny - h) % ny]
        return remote(row, row, ny_send.at[h], ny_recv.at[h], {"cols": next_col})

    norm_z = [
        remote(zbuf.at[core, z], zbuf.at[core, z], nz_send.at[i], nz_recv.at[i], {"zero": t})
        for i, t in enumerate(others)
    ]
    norm_pair = remote(zbuf.at[core], zbuf.at[core], nz_send.at[nz - 1], nz_recv.at[nz - 1], {"zero": peer})

    for c in loads[:4]:
        c.wait()
    pl.semaphore_wait(barrier, 5)
    tell(2)
    for d in range(2):
        ring(d, 0).start()
    for d in range(2):
        low(d).start()
        for i in range(1, EARLY):
            ring(d, i).start()
    for c in loads[4:]:
        c.wait()
    gain = n_in[0] + n_in[1]
    ybuf[pl.ds(col, 1)] = jnp.concatenate([gain] * ny, axis=1)[None]
    maxima(0)
    know(2)
    tell(3)
    maxima(1)
    know(3)
    tell(4)

    first = remote(pmax.at[1 - core], pget, max_send.at[0], max_recv.at[0], {"zero": peer})
    first.start()
    norm_y(0).start()
    first.wait_recv()
    cmax[...] = jnp.maximum(pmax[core], pget[...])
    know(4)
    spread = [
        remote(cmax, allmax.at[d], max_send.at[d], max_recv.at[d], {"zero": others[d - 1]}) for d in range(1, nz)
    ]
    for c in spread:
        c.start()
    for i in range(EARLY, own):
        for d in range(2):
            ring(d, i).start()
    for h in range(1, ny - 1):
        norm_y(h - 1).wait_recv()
        norm_y(h).start()
    top = cmax[...]
    for d, c in enumerate(spread):
        c.wait_recv()
        top = jnp.maximum(top, allmax[d + 1])
    col_out[pl.ds(core, 1)] = top[None]
    back = remote(col_out.at[core], col_out.at[core], max_send.at[nz], max_recv.at[nz], {"zero": peer})
    back.start()
    norm_y(ny - 2).wait_recv()
    lane = lax.broadcasted_iota(jnp.int32, (1, LANES), 1) // (LANES // ny)
    row = ybuf[0]
    for k in range(1, ny):
        row = jnp.where(lane == k, ybuf[k], row)
    zbuf[pl.ds(core, 1), pl.ds(z, 1)] = row[None, None]
    back.wait_recv()
    for m in range(2):
        for r in range(columns // LANES):
            inv[m, :, r * LANES : (r + 1) * LANES] = 1.0 / col_out[m, r : r + 1, :]

    def near(d, m):
        first_row = pl.multiple_of(block_rows(d, 1), rows)
        for t in range(columns // TILE):
            at = slice(t * TILE, (t + 1) * TILE)
            new = merged(raw.at[d, m], l_raw.at[d, m], m, at) * inv[m, :, at]
            outs[m][pl.ds(first_row, rows), at] = new.astype(jnp.bfloat16)

    def near_half(h):
        for d in range(2):
            if h == 0:
                low(d).wait_recv()
            for k in range(h * CH, (h + 1) * CH):
                ring(d, k).wait_recv()
            near(d, matrix(d, h * CH))

    mine = pl.multiple_of(zero * rows, rows)
    sent = [0, 0]

    def drain(d, i):
        while sent[d] <= i:
            ring(d, sent[d]).wait_send()
            sent[d] += 1

    def receive(d, i):
        ring(d, i).wait_recv()
        pair(d, i).start()

    for i in range(own, pieces):
        if i == own:
            near_half(0)
        if i == own + CH:
            near_half(1)
        for d in range(2):
            drain(d, i - DEPTH)
            ring(d, i).start()
            if i < 2 * own:
                pair(d, i - own).start()
        if i == own + 1:
            for c in norm_z:
                c.start()
            for m in range(2):
                for t in range(columns // TILE):
                    at = slice(t * TILE, (t + 1) * TILE)
                    outs[m][pl.ds(mine, rows), at] = (whole[m, :, at] * inv[m, :, at]).astype(jnp.bfloat16)
        if i == own + 2:
            for m in range(2):
                block = outs[m].at[pl.ds(mine, rows)]
                remote(block, block, pair_send, pair_recv.at[m, 0], {"zero": peer}).start()
        if i == 2 * own:
            for c in norm_z:
                c.wait_recv()
            norm_pair.start()
        if i - LAG >= own:
            for d in range(2):
                receive(d, i - LAG)
    for i in range(pieces - LAG, pieces):
        for d in range(2):
            receive(d, i)

    norm_pair.wait_recv()
    for k in range(nz):
        for c in range(2):
            norm_out[2 * k + c : 2 * k + c + 1, :] = zbuf[c, k]
    for d in range(2):
        low(d).wait_send()
        drain(d, pieces - 1)
    for c in [first, *spread, back, *norm_z, norm_pair]:
        c.wait_send()
    for h in range(ny - 1):
        norm_y(h).wait_send()
    for m in range(2):
        for slot in range(nz):
            block = outs[m].at[pl.ds(0, rows)]
            remote(block, block, pair_send, pair_recv.at[m, slot], {"zero": peer}).wait_recv()
    remote(og, og, pair_send, pair_recv.at[0, 0], {"zero": peer}).wait_send()


def write_out(parts, *refs):
    ins, outs, (scratch, sem) = refs[:4], refs[4:9], refs[9:]
    size = ins[0].shape[0] // parts
    copies = [
        pltpu.make_async_copy(
            ins[m].at[pl.ds(i * size, size)], outs[m].at[pl.ds(i * size, size)], sem.at[m * parts + i]
        )
        for i in range(parts)
        for m in range(2)
    ]
    copies += [pltpu.make_async_copy(ins[2].at[m], outs[2 + m], sem.at[2 * parts + m]) for m in range(2)]
    for c in copies:
        c.start()
    scratch[...] = ins[3][...].astype(jnp.bfloat16)
    last = pltpu.make_async_copy(scratch, outs[4], sem.at[2 * parts + 2])
    last.start()
    for c in copies + [last]:
        c.wait()


def per_device(weight_gate, low_gate, high_gate, weight_up, low_up, high_up, norm_train, norm_step):
    devices, ny = lax.axis_size("zero"), lax.axis_size("cols")
    nz = devices // 2
    rows, columns = weight_gate.shape
    rank = low_gate.shape[1]
    share = norm_train.shape[0]
    tiles = columns // LANES
    f32, bf16 = jnp.float32, jnp.bfloat16
    hbm = pl.BlockSpec(memory_space=pltpu.HBM)
    vmem = pl.BlockSpec(memory_space=pltpu.VMEM)
    dma = pltpu.SemaphoreType.DMA
    serving_gate, serving_up, column, norm = pl.pallas_call(
        functools.partial(kernel, nz, ny),
        out_shape=(
            pltpu.VMEM((devices * rows, columns), bf16),
            pltpu.VMEM((devices * rows, columns), bf16),
            pltpu.VMEM((2, tiles, LANES), f32),
            pltpu.VMEM((devices, LANES), f32),
        ),
        in_specs=[hbm] * 8,
        out_specs=(vmem,) * 4,
        scratch_shapes=[
            pltpu.VMEM((2, rows, columns), bf16),
            pltpu.VMEM((2, rank, rows), bf16),
            pltpu.VMEM((2, rank, columns), bf16),
            pltpu.VMEM((2, 1, share), f32),
            pltpu.VMEM((2, 2, rows, columns), bf16),
            pltpu.VMEM((2, 2, rank, rows), bf16),
            pltpu.VMEM((2, rows, columns), f32),
            pltpu.VMEM((2, tiles, LANES), f32),
            pltpu.VMEM((tiles, LANES), f32),
            pltpu.VMEM((tiles, LANES), f32),
            pltpu.VMEM((nz, tiles, LANES), f32),
            pltpu.VMEM((2, 1, columns), f32),
            pltpu.VMEM((ny, 1, LANES), f32),
            pltpu.VMEM((2, nz, 1, LANES), f32),
            dma((8,)),
            dma((2, DEPTH)),
            dma((2, (nz - 1) * CH)),
            dma((2,)),
            dma((2,)),
            dma,
            dma((2, nz)),
            dma((nz + 1,)),
            dma((nz + 1,)),
            dma((ny - 1,)),
            dma((ny - 1,)),
            dma((nz,)),
            dma((nz,)),
            pltpu.SemaphoreType.REGULAR((3,)),
        ],
        compiler_params=pltpu.CompilerParams(
            collective_id=0, has_side_effects=True, vmem_limit_bytes=47 << 20
        ),
    )(
        weight_gate, low_gate.T, high_gate, weight_up, low_up.T, high_up,
        norm_train.reshape(1, share), norm_step.reshape(1, share),
    )
    parts = 4
    serving_gate, serving_up, column_gate, column_up, norm = pl.pallas_call(
        functools.partial(write_out, parts),
        out_shape=(
            jax.ShapeDtypeStruct((devices * rows, columns), bf16),
            jax.ShapeDtypeStruct((devices * rows, columns), bf16),
            jax.ShapeDtypeStruct((tiles, LANES), f32),
            jax.ShapeDtypeStruct((tiles, LANES), f32),
            jax.ShapeDtypeStruct((devices, LANES), bf16),
        ),
        in_specs=[vmem] * 4,
        out_specs=(hbm,) * 5,
        scratch_shapes=[pltpu.VMEM((devices, LANES), bf16), dma((2 * parts + 3,))],
        compiler_params=pltpu.CompilerParams(vmem_limit_bytes=20 << 20),
    )(serving_gate, serving_up, column, norm)
    return (serving_gate, serving_up, column_gate.reshape(-1), column_up.reshape(-1), norm.reshape(-1))


def solution(mesh):
    in_specs = (
        P(("job", "zero"), "cols"),
        P(("job", "zero"), None),
        P("job", "cols"),
        P(("job", "zero"), "cols"),
        P(("job", "zero"), None),
        P("job", "cols"),
        P(("job", "zero", "cols")),
        P(("job", "zero", "cols")),
    )
    out_specs = (
        P("job", "cols"),
        P("job", "cols"),
        P(("job", "cols")),
        P(("job", "cols")),
        P("job"),
    )
    return jax.shard_map(
        per_device, mesh=mesh, in_specs=in_specs, out_specs=out_specs, check_vma=False
    )
```

time: 101 us -> 101 us (level)
  no operation moved by 1% of the time
where the time goes in v3:
time: 101 us; the launch traced here: 100 us
  Pallas kernels  99.8 us (99%)
    pallas_call x1, Pallas kernels, per_device(): pl.pallas_call(functools.partial(kernel, nz, ny), out_shape=(pltpu.VMEM((...  93.8 us
    pallas_call x1, Pallas kernels, per_device(): pl.pallas_call(functools.partial(write_out, parts), out_shape=(jax.ShapeD...  5.96 us

profile of v3, /device:TPU:1, one launch (start us, length us, event | category | flops | bytes accessed | tf_op | source)
XLA Modules:
  0.0 100.4 jit_solution(3510897437217136496)
XLA Ops:
  0.6 93.8 %shard_map.119 = (bf16[2048,2048]{1,0:T(8,128)(2,1)S(1)}, bf16[2048,2048]{1,0:T(8,128)(2,1)S(1)}, f32[2,16,128]{2,1,0:T(8,128)S(1)}, f32[16,128]{1,0:T(8,128)S(1)}) custom-call(bf16[128,2048]{1,0:T(8,128)(2,1)} %wg_hbm.1, bf16[32,128]{1,0:T(8,128)(2,1)} %bitcast.7, bf16[32,2048]{1,0:T(8,128)(2,1)} %hg_hbm.1, bf16[128,2048]{1,0:T(8,128)(2,1)} %wu_hbm.1, ...), custom_call_target="tpu_custom_call" | custom-call | tf_op jit(solution)/shard_map/pallas_call | solution.py:290
  94.4 6.0 %shard_map.120 = (bf16[2048,2048]{1,0:T(8,128)(2,1)}, bf16[2048,2048]{1,0:T(8,128)(2,1)}, f32[16,128]{1,0:T(8,128)}, f32[16,128]{1,0:T(8,128)}, bf16[16,128]{1,0:T(8,128)(2,1)}) custom-call(bf16[2048,2048]{1,0:T(8,128)(2,1)S(1)} %get-tuple-element.14.refs_0_, bf16[2048,2048]{1,0:T(8,128)(2,1)S(1)} %get-tuple-element.15.refs_1_, ...), custom_call_target="tpu_custom_call" | custom-call | tf_op jit(solution)/shard_map/pallas_call | solution.py:338

commit v4 on v3

--- a/solution.py
+++ b/solution.py
@@ -13,7 +13,7 @@
 TILE = 512
 DEPTH = 8
 LAG = 6
-EARLY = 3
+EARLY = (4, 2)
 LANES = 128
 
 
@@ -28,7 +28,7 @@
     wg_hbm, lg_hbm, hg_hbm, wu_hbm, lu_hbm, hu_hbm, nt_hbm, ns_hbm,
     og, ou, col_out, norm_out,
     w_in, l_in, h_in, n_in, raw, l_raw, whole, pmax, pget, cmax, allmax, inv, ybuf, zbuf,
-    in_sem, ring_send, ring_recv, low_send, low_recv, pair_send, pair_recv,
+    in_sem, ring_send, ring_recv, rest_send, rest_recv, low_send, low_recv, pair_send, pair_recv,
     max_send, max_recv, ny_send, ny_recv, nz_send, nz_recv, known,
 ):
     zero, col = lax.axis_index("zero"), lax.axis_index("cols")
@@ -56,11 +56,16 @@
     peer = zero + 1 - 2 * core
     to = ((z + 1) % nz * 2 + core, (z + nz - 1) % nz * 2 + core)
     others = [(z + d) % nz * 2 + core for d in range(1, nz)]
-    next_col, last_col = (col + 1) % ny, (col + ny - 1) % ny
     for t in (*to, peer):
         pl.semaphore_signal(barrier, 1, device_id={"zero": t}, device_id_type=MESH)
-    for t in (next_col, last_col):
-        pl.semaphore_signal(barrier, 1, device_id={"cols": t}, device_id_type=MESH)
+    sides = (col + 1 < ny, col > 0)
+    beside = (lax.rem(col + 1, ny), lax.rem(col + ny - 1, ny))
+    for e in range(2):
+
+        @pl.when(sides[e])
+        def _():
+            pl.semaphore_signal(barrier, 1, device_id={"cols": beside[e]}, device_id_type=MESH)
+
 
     def know(hops):
         pl.semaphore_wait(known.at[hops - 2], 2)
@@ -91,14 +96,31 @@
     def matrix(d, k):
         return k // CH if d == 0 else 1 - k // CH
 
+    def chunk(k):
+        return k * step_rows if k < CH else (own - 1 - k) * step_rows
+
+    split = step_rows // 2
+
     def piece(d, i, hops):
-        k = i % own
-        at = pl.multiple_of(block_rows(d, i // own + hops) + k % CH * step_rows, step_rows)
-        return outs[matrix(d, k)].at[pl.ds(at, step_rows)]
+        size = step_rows - split if (d, i) == (0, pieces - 1) else step_rows
+        at = pl.multiple_of(block_rows(d, i // own + hops) + chunk(i % own), split)
+        return outs[matrix(d, i % own)].at[pl.ds(at, size)]
+
+    def rest(d, hops):
+        at = pl.multiple_of(block_rows(d, half - 1 + hops) + chunk(CH - 1) + step_rows - split, split)
+        return og.at[pl.ds(at, split)]
+
+    def rest_ring(d):
+        ref = rest(d, 0)
+        return remote(ref, ref, rest_send.at[d], rest_recv.at[d], {"zero": to[d]})
+
+    def rest_pair(d):
+        ref = rest(d, 1)
+        return remote(ref, ref, pair_send, pair_recv.at[0, half], {"zero": peer})
 
     def ring(d, i):
         if i < own:
-            m, at = matrix(d, i), pl.ds(i % CH * step_rows, step_rows)
+            m, at = matrix(d, i), pl.ds(chunk(i), step_rows)
             src, dst = w_in.at[m, at], raw.at[d, m, at]
         else:
             src = dst = piece(d, i, 0)
@@ -113,9 +135,29 @@
     def low(d):
         return remote(l_in, l_raw.at[d], low_send.at[d], low_recv.at[d], {"zero": to[d]})
 
-    def norm_y(h):
-        row = ybuf.at[(col + ny - h) % ny]
-        return remote(row, row, ny_send.at[h], ny_recv.at[h], {"cols": next_col})
+    def norm_y(e, h):
+        row = ybuf.at[lax.rem(col + ny - h, ny) if e == 0 else lax.rem(col + h, ny)]
+        return remote(row, row, ny_send.at[e, h], ny_recv.at[e, h], {"cols": beside[e]})
+
+    def gives(e, h):
+        return (sides[0] & (col >= h), sides[1] & (col + h < ny))[e]
+
+    def gets(e, h):
+        return (col >= h + 1, col + h + 1 < ny)[e]
+
+    def norm_y_start(h):
+        for e in range(2):
+
+            @pl.when(gives(e, h))
+            def _():
+                norm_y(e, h).start()
+
+    def norm_y_get(h):
+        for e in range(2):
+
+            @pl.when(gets(e, h))
+            def _():
+                norm_y(e, h).wait_recv()
 
     norm_z = [
         remote(zbuf.at[core, z], zbuf.at[core, z], nz_send.at[i], nz_recv.at[i], {"zero": t})
@@ -125,14 +167,21 @@
 
     for c in loads[:4]:
         c.wait()
-    pl.semaphore_wait(barrier, 5)
+    pl.semaphore_wait(barrier, 3 + sides[0].astype(jnp.int32) + sides[1].astype(jnp.int32))
     tell(2)
     for d in range(2):
         ring(d, 0).start()
     for d in range(2):
         low(d).start()
-        for i in range(1, EARLY):
+        for i in range(1, EARLY[1]):
             ring(d, i).start()
+
+    def between():
+        for i in range(EARLY[1], EARLY[0]):
+            for d in range(2):
+                ring(d, i).start()
+
+    pl.when(z < half)(between)
     for c in loads[4:]:
         c.wait()
     gain = n_in[0] + n_in[1]
@@ -146,7 +195,7 @@
 
     first = remote(pmax.at[1 - core], pget, max_send.at[0], max_recv.at[0], {"zero": peer})
     first.start()
-    norm_y(0).start()
+    norm_y_start(0)
     first.wait_recv()
     cmax[...] = jnp.maximum(pmax[core], pget[...])
     know(4)
@@ -155,12 +204,13 @@
     ]
     for c in spread:
         c.start()
-    for i in range(EARLY, own):
+    pl.when(z >= half)(between)
+    for i in range(EARLY[0], own):
         for d in range(2):
             ring(d, i).start()
     for h in range(1, ny - 1):
-        norm_y(h - 1).wait_recv()
-        norm_y(h).start()
+        norm_y_get(h - 1)
+        norm_y_start(h)
     top = cmax[...]
     for d, c in enumerate(spread):
         c.wait_recv()
@@ -168,7 +218,7 @@
     col_out[pl.ds(core, 1)] = top[None]
     back = remote(col_out.at[core], col_out.at[core], max_send.at[nz], max_recv.at[nz], {"zero": peer})
     back.start()
-    norm_y(ny - 2).wait_recv()
+    norm_y_get(ny - 2)
     lane = lax.broadcasted_iota(jnp.int32, (1, LANES), 1) // (LANES // ny)
     row = ybuf[0]
     for k in range(1, ny):
@@ -234,9 +284,18 @@
         if i - LAG >= own:
             for d in range(2):
                 receive(d, i - LAG)
+    pl.when(z != nz - 1)(lambda: rest_ring(0).start())
+    pl.when(z == 1)(lambda: rest_ring(1).start())
     for i in range(pieces - LAG, pieces):
         for d in range(2):
             receive(d, i)
+    for d, here in ((0, z != 0), (1, z == 0)):
+
+        @pl.when(here)
+        def _():
+            rest_ring(d).wait_recv()
+            rest_pair(d).start()
+
 
     norm_pair.wait_recv()
     for k in range(nz):
@@ -248,7 +307,14 @@
     for c in [first, *spread, back, *norm_z, norm_pair]:
         c.wait_send()
     for h in range(ny - 1):
-        norm_y(h).wait_send()
+        for e in range(2):
+
+            @pl.when(gives(e, h))
+            def _():
+                norm_y(e, h).wait_send()
+
+    pl.when(z != nz - 1)(lambda: rest_ring(0).wait_send())
+    pl.when(z == 1)(lambda: rest_ring(1).wait_send())
     for m in range(2):
         for slot in range(nz):
             block = outs[m].at[pl.ds(0, rows)]
@@ -317,12 +383,14 @@
             dma((2, (nz - 1) * CH)),
             dma((2,)),
             dma((2,)),
+            dma((2,)),
+            dma((2,)),
             dma,
             dma((2, nz)),
             dma((nz + 1,)),
             dma((nz + 1,)),
-            dma((ny - 1,)),
-            dma((ny - 1,)),
+            dma((2, ny - 1)),
+            dma((2, ny - 1)),
             dma((nz,)),
             dma((nz,)),
             pltpu.SemaphoreType.REGULAR((3,)),

time: 101 us -> 97.8 us (0.968)
  Pallas kernels: 99.8 us -> 97 us
    pallas_call x1, Pallas kernels: 93.8 us -> 91.1 us  [per_device(): pl.pallas_call(functools.partial(kernel, nz, ny), out_shape=(pltpu.VMEM((...]
where the time goes in v4:
time: 97.8 us; the launch traced here: 97.7 us
  Pallas kernels  97 us (99%)
    pallas_call x1, Pallas kernels, per_device(): pl.pallas_call(functools.partial(kernel, nz, ny), out_shape=(pltpu.VMEM((...  91.1 us
    pallas_call x1, Pallas kernels, per_device(): pl.pallas_call(functools.partial(write_out, parts), out_shape=(jax.ShapeD...  5.96 us

profile of v4, /device:TPU:1, one launch (start us, length us, event | category | flops | bytes accessed | tf_op | source)
XLA Modules:
  0.0 97.7 jit_solution(5443063555846125011)
XLA Ops:
  0.6 91.1 %shard_map.119 = (bf16[2048,2048]{1,0:T(8,128)(2,1)S(1)}, bf16[2048,2048]{1,0:T(8,128)(2,1)S(1)}, f32[2,16,128]{2,1,0:T(8,128)S(1)}, f32[16,128]{1,0:T(8,128)S(1)}) custom-call(bf16[128,2048]{1,0:T(8,128)(2,1)} %wg_hbm.1, bf16[32,128]{1,0:T(8,128)(2,1)} %bitcast.7, bf16[32,2048]{1,0:T(8,128)(2,1)} %hg_hbm.1, bf16[128,2048]{1,0:T(8,128)(2,1)} %wu_hbm.1, ...), custom_call_target="tpu_custom_call" | custom-call | tf_op jit(solution)/shard_map/pallas_call | solution.py:356
  91.7 6.0 %shard_map.120 = (bf16[2048,2048]{1,0:T(8,128)(2,1)}, bf16[2048,2048]{1,0:T(8,128)(2,1)}, f32[16,128]{1,0:T(8,128)}, f32[16,128]{1,0:T(8,128)}, bf16[16,128]{1,0:T(8,128)(2,1)}) custom-call(bf16[2048,2048]{1,0:T(8,128)(2,1)S(1)} %get-tuple-element.14.refs_0_, bf16[2048,2048]{1,0:T(8,128)(2,1)S(1)} %get-tuple-element.15.refs_1_, ...), custom_call_target="tpu_custom_call" | custom-call | tf_op jit(solution)/shard_map/pallas_call | solution.py:406

commit v5 on v4

--- a/solution.py
+++ b/solution.py
@@ -13,7 +13,7 @@
 TILE = 512
 DEPTH = 8
 LAG = 6
-EARLY = (4, 2)
+EARLY = (4, 3)
 LANES = 128
 
 
@@ -29,7 +29,7 @@
     og, ou, col_out, norm_out,
     w_in, l_in, h_in, n_in, raw, l_raw, whole, pmax, pget, cmax, allmax, inv, ybuf, zbuf,
     in_sem, ring_send, ring_recv, rest_send, rest_recv, low_send, low_recv, pair_send, pair_recv,
-    max_send, max_recv, ny_send, ny_recv, nz_send, nz_recv, known,
+    max_send, max_recv, ny_send, ny_recv, nz_send, nz_recv, known, answer,
 ):
     zero, col = lax.axis_index("zero"), lax.axis_index("cols")
     z, core = zero // 2, zero % 2
@@ -56,16 +56,25 @@
     peer = zero + 1 - 2 * core
     to = ((z + 1) % nz * 2 + core, (z + nz - 1) % nz * 2 + core)
     others = [(z + d) % nz * 2 + core for d in range(1, nz)]
-    for t in (*to, peer):
-        pl.semaphore_signal(barrier, 1, device_id={"zero": t}, device_id_type=MESH)
     sides = (col + 1 < ny, col > 0)
     beside = (lax.rem(col + 1, ny), lax.rem(col + ny - 1, ny))
-    for e in range(2):
-
-        @pl.when(sides[e])
-        def _():
-            pl.semaphore_signal(barrier, 1, device_id={"cols": beside[e]}, device_id_type=MESH)
-
+
+    def signal(sem, axis, index):
+        pl.semaphore_signal(sem, 1, device_id={axis: index}, device_id_type=MESH)
+
+    low_end, high_end = z == 0, z == nz - 1
+    pl.when(z < nz - 2)(lambda: signal(barrier, "zero", to[0]))
+    pl.when(low_end | high_end)(lambda: signal(barrier, "zero", to[1]))
+    pl.when(core == 1)(lambda: signal(barrier, "zero", peer))
+    pl.when(sides[0])(lambda: signal(barrier, "cols", beside[0]))
+
+    def greeted():
+        count = sum(c.astype(jnp.int32) for c in (z > 0, z == nz - 2, core == 0, sides[1]))
+        pl.when(count > 0)(lambda: pl.semaphore_wait(barrier, count))
+        pl.when((z > 0) & (z < nz - 1))(lambda: signal(answer.at[0], "zero", to[1]))
+        pl.when(z >= nz - 2)(lambda: signal(answer.at[1], "zero", to[0]))
+        pl.when(core == 0)(lambda: signal(answer.at[2], "zero", peer))
+        pl.when(sides[1])(lambda: signal(answer.at[3], "cols", beside[1]))
 
     def know(hops):
         pl.semaphore_wait(known.at[hops - 2], 2)
@@ -121,7 +130,8 @@
     def ring(d, i):
         if i < own:
             m, at = matrix(d, i), pl.ds(chunk(i), step_rows)
-            src, dst = w_in.at[m, at], raw.at[d, m, at]
+            src = (wg_hbm, wu_hbm)[m].at[at] if i < EARLY[1] else w_in.at[m, at]
+            dst = raw.at[d, m, at]
         else:
             src = dst = piece(d, i, 0)
         return remote(src, dst, ring_send.at[d, i % DEPTH], ring_recv.at[d, i], {"zero": to[d]})
@@ -165,15 +175,10 @@
     ]
     norm_pair = remote(zbuf.at[core], zbuf.at[core], nz_send.at[nz - 1], nz_recv.at[nz - 1], {"zero": peer})
 
-    for c in loads[:4]:
-        c.wait()
-    pl.semaphore_wait(barrier, 3 + sides[0].astype(jnp.int32) + sides[1].astype(jnp.int32))
-    tell(2)
-    for d in range(2):
-        ring(d, 0).start()
-    for d in range(2):
-        low(d).start()
-        for i in range(1, EARLY[1]):
+    greeted()
+
+    def begin(d):
+        for i in range(EARLY[1]):
             ring(d, i).start()
 
     def between():
@@ -181,21 +186,46 @@
             for d in range(2):
                 ring(d, i).start()
 
-    pl.when(z < half)(between)
-    for c in loads[4:]:
+    pl.when((z > 0) & (z < nz - 1))(lambda: begin(1))
+    pl.when(z < nz - 2)(lambda: pl.semaphore_wait(answer.at[0], 1))
+    begin(0)
+
+    @pl.when(high_end)
+    def _():
+        pl.semaphore_wait(answer.at[1], 1)
+        begin(1)
+
+    pl.when(z > 0)(lambda: tell(2))
+    for c in loads:
         c.wait()
+    pl.when((z > 0) & (z < half))(between)
     gain = n_in[0] + n_in[1]
     ybuf[pl.ds(col, 1)] = jnp.concatenate([gain] * ny, axis=1)[None]
     maxima(0)
+
+    @pl.when(low_end)
+    def _():
+        for i in range(EARLY[1], EARLY[0]):
+            ring(0, i).start()
+        pl.semaphore_wait(answer.at[1], 1)
+        tell(2)
+        begin(1)
+        for i in range(EARLY[1], EARLY[0]):
+            ring(1, i).start()
+
+    for d in range(2):
+        low(d).start()
+    maxima(1)
     know(2)
     tell(3)
-    maxima(1)
-    know(3)
-    tell(4)
+    pl.when(core == 1)(lambda: pl.semaphore_wait(answer.at[2], 1))
+    pl.when(sides[0])(lambda: pl.semaphore_wait(answer.at[3], 1))
 
     first = remote(pmax.at[1 - core], pget, max_send.at[0], max_recv.at[0], {"zero": peer})
     first.start()
     norm_y_start(0)
+    know(3)
+    tell(4)
     first.wait_recv()
     cmax[...] = jnp.maximum(pmax[core], pget[...])
     know(4)
@@ -286,24 +316,12 @@
                 receive(d, i - LAG)
     pl.when(z != nz - 1)(lambda: rest_ring(0).start())
     pl.when(z == 1)(lambda: rest_ring(1).start())
-    for i in range(pieces - LAG, pieces):
-        for d in range(2):
-            receive(d, i)
-    for d, here in ((0, z != 0), (1, z == 0)):
-
-        @pl.when(here)
-        def _():
-            rest_ring(d).wait_recv()
-            rest_pair(d).start()
-
-
     norm_pair.wait_recv()
     for k in range(nz):
         for c in range(2):
             norm_out[2 * k + c : 2 * k + c + 1, :] = zbuf[c, k]
     for d in range(2):
         low(d).wait_send()
-        drain(d, pieces - 1)
     for c in [first, *spread, back, *norm_z, norm_pair]:
         c.wait_send()
     for h in range(ny - 1):
@@ -313,12 +331,32 @@
             def _():
                 norm_y(e, h).wait_send()
 
+    def pair_got(m, slot):
+        block = outs[m].at[pl.ds(0, rows)]
+        remote(block, block, pair_send, pair_recv.at[m, slot], {"zero": peer}).wait_recv()
+
+    early = [(m, slot) for m in range(2) for slot in range(nz) if slot not in (half - 1, half, half + 1)]
+    for m, slot in early:
+        pair_got(m, slot)
+    for i in range(pieces - LAG, pieces):
+        for d in range(2):
+            receive(d, i)
+    for d, here in ((0, z != 0), (1, z == 0)):
+
+        @pl.when(here)
+        def _():
+            rest_ring(d).wait_recv()
+            rest_pair(d).start()
+
+
+    for slot in (half - 1, half, half + 1):
+        for m in range(2):
+            if (m, slot) not in early:
+                pair_got(m, slot)
+    for d in range(2):
+        drain(d, pieces - 1)
     pl.when(z != nz - 1)(lambda: rest_ring(0).wait_send())
     pl.when(z == 1)(lambda: rest_ring(1).wait_send())
-    for m in range(2):
-        for slot in range(nz):
-            block = outs[m].at[pl.ds(0, rows)]
-            remote(block, block, pair_send, pair_recv.at[m, slot], {"zero": peer}).wait_recv()
     remote(og, og, pair_send, pair_recv.at[0, 0], {"zero": peer}).wait_send()
 
 
@@ -394,6 +432,7 @@
             dma((nz,)),
             dma((nz,)),
             pltpu.SemaphoreType.REGULAR((3,)),
+            pltpu.SemaphoreType.REGULAR((4,)),
         ],
         compiler_params=pltpu.CompilerParams(
             collective_id=0, has_side_effects=True, vmem_limit_bytes=47 << 20

time: 97.8 us -> 96.8 us (0.990)
  no operation moved by 1% of the time
where the time goes in v5:
time: 96.8 us; the launch traced here: 96.7 us
  Pallas kernels  96.1 us (99%)
    pallas_call x1, Pallas kernels, per_device(): pl.pallas_call(functools.partial(kernel, nz, ny), out_shape=(pltpu.VMEM((...  90.1 us
    pallas_call x1, Pallas kernels, per_device(): pl.pallas_call(functools.partial(write_out, parts), out_shape=(jax.ShapeD...  5.96 us

profile of v5, /device:TPU:1, one launch (start us, length us, event | category | flops | bytes accessed | tf_op | source)
XLA Modules:
  0.0 96.7 jit_solution(13473908481053296724)
XLA Ops:
  0.6 90.1 %shard_map.119 = (bf16[2048,2048]{1,0:T(8,128)(2,1)S(1)}, bf16[2048,2048]{1,0:T(8,128)(2,1)S(1)}, f32[2,16,128]{2,1,0:T(8,128)S(1)}, f32[16,128]{1,0:T(8,128)S(1)}) custom-call(bf16[128,2048]{1,0:T(8,128)(2,1)} %wg_hbm.1, bf16[32,128]{1,0:T(8,128)(2,1)} %bitcast.7, bf16[32,2048]{1,0:T(8,128)(2,1)} %hg_hbm.1, bf16[128,2048]{1,0:T(8,128)(2,1)} %wu_hbm.1, ...), custom_call_target="tpu_custom_call" | custom-call | tf_op jit(solution)/shard_map/pallas_call | solution.py:394
  90.8 6.0 %shard_map.120 = (bf16[2048,2048]{1,0:T(8,128)(2,1)}, bf16[2048,2048]{1,0:T(8,128)(2,1)}, f32[16,128]{1,0:T(8,128)}, f32[16,128]{1,0:T(8,128)}, bf16[16,128]{1,0:T(8,128)(2,1)}) custom-call(bf16[2048,2048]{1,0:T(8,128)(2,1)S(1)} %get-tuple-element.14.refs_0_, bf16[2048,2048]{1,0:T(8,128)(2,1)S(1)} %get-tuple-element.15.refs_1_, ...), custom_call_target="tpu_custom_call" | custom-call | tf_op jit(solution)/shard_map/pallas_call | solution.py:445

commit v6 on v5

--- a/solution.py
+++ b/solution.py
@@ -13,7 +13,7 @@
 TILE = 512
 DEPTH = 8
 LAG = 6
-EARLY = (4, 3)
+EARLY = (3, 2)
 LANES = 128
 
 
@@ -27,7 +27,7 @@
     nz, ny,
     wg_hbm, lg_hbm, hg_hbm, wu_hbm, lu_hbm, hu_hbm, nt_hbm, ns_hbm,
     og, ou, col_out, norm_out,
-    w_in, l_in, h_in, n_in, raw, l_raw, whole, pmax, pget, cmax, allmax, inv, ybuf, zbuf,
+    w_in, l_in, h_in, n_in, raw, l_raw, whole, pmax, pget, cmax, cnear, allmax, inv, ybuf, zbuf,
     in_sem, ring_send, ring_recv, rest_send, rest_recv, low_send, low_recv, pair_send, pair_recv,
     max_send, max_recv, ny_send, ny_recv, nz_send, nz_recv, known, answer,
 ):
@@ -108,24 +108,27 @@
     def chunk(k):
         return k * step_rows if k < CH else (own - 1 - k) * step_rows
 
-    split = step_rows // 2
+    split = step_rows // 4 * 3
 
     def piece(d, i, hops):
-        size = step_rows - split if (d, i) == (0, pieces - 1) else step_rows
-        at = pl.multiple_of(block_rows(d, i // own + hops) + chunk(i % own), split)
+        size = step_rows - split if i == pieces - 1 else step_rows
+        at = pl.multiple_of(block_rows(d, i // own + hops) + chunk(i % own), step_rows // 4)
         return outs[matrix(d, i % own)].at[pl.ds(at, size)]
 
-    def rest(d, hops):
-        at = pl.multiple_of(block_rows(d, half - 1 + hops) + chunk(CH - 1) + step_rows - split, split)
-        return og.at[pl.ds(at, split)]
-
-    def rest_ring(d):
-        ref = rest(d, 0)
-        return remote(ref, ref, rest_send.at[d], rest_recv.at[d], {"zero": to[d]})
-
-    def rest_pair(d):
-        ref = rest(d, 1)
-        return remote(ref, ref, pair_send, pair_recv.at[0, half], {"zero": peer})
+    def rest(via, m, hops):
+        first_row = block_rows(via, half - 1 + hops) + chunk(CH - 1) + step_rows - split
+        return outs[m].at[pl.ds(pl.multiple_of(first_row, step_rows // 4), split)]
+
+    def rest_ring(via, m):
+        ref = rest(via, m, 0)
+        return remote(ref, ref, rest_send.at[via, m], rest_recv.at[via, m], {"zero": to[via]})
+
+    def rest_pair(via, m):
+        ref = rest(via, m, 1)
+        return remote(ref, ref, pair_send, pair_recv.at[m, half], {"zero": peer})
+
+    rest_out = ((0, 0, z != nz - 1), (1, 0, z == 1), (1, 1, z != half), (0, 1, z == half - 2))
+    rest_in = ((0, 0, z != 0), (1, 0, z == 0), (1, 1, z != half - 1), (0, 1, z == half - 1))
 
     def ring(d, i):
         if i < own:
@@ -181,10 +184,9 @@
         for i in range(EARLY[1]):
             ring(d, i).start()
 
-    def between():
-        for i in range(EARLY[1], EARLY[0]):
-            for d in range(2):
-                ring(d, i).start()
+    def more(d, first, last):
+        for i in range(first, last):
+            ring(d, i).start()
 
     pl.when((z > 0) & (z < nz - 1))(lambda: begin(1))
     pl.when(z < nz - 2)(lambda: pl.semaphore_wait(answer.at[0], 1))
@@ -198,20 +200,17 @@
     pl.when(z > 0)(lambda: tell(2))
     for c in loads:
         c.wait()
-    pl.when((z > 0) & (z < half))(between)
+    pl.when(z < half)(lambda: more(0, *EARLY[::-1]))
+    pl.when((z > 0) & (z < half))(lambda: more(1, *EARLY[::-1]))
     gain = n_in[0] + n_in[1]
     ybuf[pl.ds(col, 1)] = jnp.concatenate([gain] * ny, axis=1)[None]
     maxima(0)
 
     @pl.when(low_end)
     def _():
-        for i in range(EARLY[1], EARLY[0]):
-            ring(0, i).start()
         pl.semaphore_wait(answer.at[1], 1)
         tell(2)
         begin(1)
-        for i in range(EARLY[1], EARLY[0]):
-            ring(1, i).start()
 
     for d in range(2):
         low(d).start()
@@ -224,27 +223,42 @@
     first = remote(pmax.at[1 - core], pget, max_send.at[0], max_recv.at[0], {"zero": peer})
     first.start()
     norm_y_start(0)
-    know(3)
-    tell(4)
     first.wait_recv()
     cmax[...] = jnp.maximum(pmax[core], pget[...])
-    know(4)
-    spread = [
-        remote(cmax, allmax.at[d], max_send.at[d], max_recv.at[d], {"zero": others[d - 1]}) for d in range(1, nz)
-    ]
-    for c in spread:
+    step_one = [remote(cmax, allmax.at[d], max_send.at[1 + d], max_recv.at[1 + d], {"zero": to[d]}) for d in range(2)]
+    far = (others[2], others[nz - 4])
+    step_two = [remote(cnear, allmax.at[2 + d], max_send.at[3 + d], max_recv.at[3 + d], {"zero": far[d]}) for d in range(2)]
+    spread = step_one + step_two
+    for c in step_one:
         c.start()
-    pl.when(z >= half)(between)
-    for i in range(EARLY[0], own):
-        for d in range(2):
-            ring(d, i).start()
+
+    def gap(d, early):
+        more(d, early, early + 1)
+
+    def fill(d, early):
+        more(d, early + 1, own)
+
+    def by_start(what):
+        pl.when(z < half)(lambda: what(0, EARLY[0]))
+        pl.when(z >= half)(lambda: what(0, EARLY[1]))
+        pl.when((z > 0) & (z < half))(lambda: what(1, EARLY[0]))
+        pl.when((z >= half) | low_end)(lambda: what(1, EARLY[1]))
+
+    by_start(gap)
+    know(3)
+    for c in step_one:
+        c.wait_recv()
+    cnear[...] = jnp.maximum(jnp.maximum(cmax[...], allmax[0]), allmax[1])
+    for c in step_two:
+        c.start()
+    by_start(fill)
     for h in range(1, ny - 1):
         norm_y_get(h - 1)
         norm_y_start(h)
-    top = cmax[...]
-    for d, c in enumerate(spread):
+    top = cnear[...]
+    for d, c in enumerate(step_two):
         c.wait_recv()
-        top = jnp.maximum(top, allmax[d + 1])
+        top = jnp.maximum(top, allmax[2 + d])
     col_out[pl.ds(core, 1)] = top[None]
     back = remote(col_out.at[core], col_out.at[core], max_send.at[nz], max_recv.at[nz], {"zero": peer})
     back.start()
@@ -259,20 +273,13 @@
         for r in range(columns // LANES):
             inv[m, :, r * LANES : (r + 1) * LANES] = 1.0 / col_out[m, r : r + 1, :]
 
-    def near(d, m):
-        first_row = pl.multiple_of(block_rows(d, 1), rows)
+    def near(d, k):
+        m, part = matrix(d, k), slice(chunk(k), chunk(k) + step_rows)
+        first_row = pl.multiple_of(block_rows(d, 1) + chunk(k), step_rows)
         for t in range(columns // TILE):
             at = slice(t * TILE, (t + 1) * TILE)
-            new = merged(raw.at[d, m], l_raw.at[d, m], m, at) * inv[m, :, at]
-            outs[m][pl.ds(first_row, rows), at] = new.astype(jnp.bfloat16)
-
-    def near_half(h):
-        for d in range(2):
-            if h == 0:
-                low(d).wait_recv()
-            for k in range(h * CH, (h + 1) * CH):
-                ring(d, k).wait_recv()
-            near(d, matrix(d, h * CH))
+            new = merged(raw.at[d, m, part], l_raw.at[d, m, :, part], m, at) * inv[m, :, at]
+            outs[m][pl.ds(first_row, step_rows), at] = new.astype(jnp.bfloat16)
 
     mine = pl.multiple_of(zero * rows, rows)
     sent = [0, 0]
@@ -287,10 +294,12 @@
         pair(d, i).start()
 
     for i in range(own, pieces):
-        if i == own:
-            near_half(0)
-        if i == own + CH:
-            near_half(1)
+        if i < 2 * own:
+            for d in range(2):
+                if i == own:
+                    low(d).wait_recv()
+                ring(d, i - own).wait_recv()
+                near(d, i - own)
         for d in range(2):
             drain(d, i - DEPTH)
             ring(d, i).start()
@@ -314,8 +323,8 @@
         if i - LAG >= own:
             for d in range(2):
                 receive(d, i - LAG)
-    pl.when(z != nz - 1)(lambda: rest_ring(0).start())
-    pl.when(z == 1)(lambda: rest_ring(1).start())
+    for via, m, here in rest_out:
+        pl.when(here)(lambda: rest_ring(via, m).start())
     norm_pair.wait_recv()
     for k in range(nz):
         for c in range(2):
@@ -341,12 +350,12 @@
     for i in range(pieces - LAG, pieces):
         for d in range(2):
             receive(d, i)
-    for d, here in ((0, z != 0), (1, z == 0)):
+    for via, m, here in rest_in:
 
         @pl.when(here)
         def _():
-            rest_ring(d).wait_recv()
-            rest_pair(d).start()
+            rest_ring(via, m).wait_recv()
+            rest_pair(via, m).start()
 
 
     for slot in (half - 1, half, half + 1):
@@ -355,8 +364,8 @@
                 pair_got(m, slot)
     for d in range(2):
         drain(d, pieces - 1)
-    pl.when(z != nz - 1)(lambda: rest_ring(0).wait_send())
-    pl.when(z == 1)(lambda: rest_ring(1).wait_send())
+    for via, m, here in rest_out:
+        pl.when(here)(lambda: rest_ring(via, m).wait_send())
     remote(og, og, pair_send, pair_recv.at[0, 0], {"zero": peer}).wait_send()
 
 
@@ -412,15 +421,16 @@
             pltpu.VMEM((2, tiles, LANES), f32),
             pltpu.VMEM((tiles, LANES), f32),
             pltpu.VMEM((tiles, LANES), f32),
-            pltpu.VMEM((nz, tiles, LANES), f32),
+            pltpu.VMEM((tiles, LANES), f32),
+            pltpu.VMEM((4, tiles, LANES), f32),
             pltpu.VMEM((2, 1, columns), f32),
             pltpu.VMEM((ny, 1, LANES), f32),
             pltpu.VMEM((2, nz, 1, LANES), f32),
             dma((8,)),
             dma((2, DEPTH)),
             dma((2, (nz - 1) * CH)),
-            dma((2,)),
-            dma((2,)),
+            dma((2, 2)),
+            dma((2, 2)),
             dma((2,)),
             dma((2,)),
             dma,
@@ -431,7 +441,7 @@
             dma((2, ny - 1)),
             dma((nz,)),
             dma((nz,)),
-            pltpu.SemaphoreType.REGULAR((3,)),
+            pltpu.SemaphoreType.REGULAR((2,)),
             pltpu.SemaphoreType.REGULAR((4,)),
         ],
         compiler_params=pltpu.CompilerParams(

time: 96.8 us -> 95.4 us (0.986)
  Pallas kernels: 96.1 us -> 94.7 us
    pallas_call x1, Pallas kernels: 90.1 us -> 88.8 us  [per_device(): pl.pallas_call(functools.partial(kernel, nz, ny), out_shape=(pltpu.VMEM((...]
where the time goes in v6:
time: 95.4 us
  Pallas kernels  94.7 us (99%)
    pallas_call x1, Pallas kernels, per_device(): pl.pallas_call(functools.partial(kernel, nz, ny), out_shape=(pltpu.VMEM((...  88.8 us
    pallas_call x1, Pallas kernels, per_device(): pl.pallas_call(functools.partial(write_out, parts), out_shape=(jax.ShapeD...  5.96 us

profile of v6, /device:TPU:1, one launch (start us, length us, event | category | flops | bytes accessed | tf_op | source)
XLA Modules:
  0.0 95.4 jit_solution(12550849790931810084)
XLA Ops:
  0.6 88.8 %shard_map.119 = (bf16[2048,2048]{1,0:T(8,128)(2,1)S(1)}, bf16[2048,2048]{1,0:T(8,128)(2,1)S(1)}, f32[2,16,128]{2,1,0:T(8,128)S(1)}, f32[16,128]{1,0:T(8,128)S(1)}) custom-call(bf16[128,2048]{1,0:T(8,128)(2,1)} %wg_hbm.1, bf16[32,128]{1,0:T(8,128)(2,1)} %bitcast.7, bf16[32,2048]{1,0:T(8,128)(2,1)} %hg_hbm.1, bf16[128,2048]{1,0:T(8,128)(2,1)} %wu_hbm.1, ...), custom_call_target="tpu_custom_call" | custom-call | tf_op jit(solution)/shard_map/pallas_call | solution.py:403
  89.4 6.0 %shard_map.120 = (bf16[2048,2048]{1,0:T(8,128)(2,1)}, bf16[2048,2048]{1,0:T(8,128)(2,1)}, f32[16,128]{1,0:T(8,128)}, f32[16,128]{1,0:T(8,128)}, bf16[16,128]{1,0:T(8,128)(2,1)}) custom-call(bf16[2048,2048]{1,0:T(8,128)(2,1)S(1)} %get-tuple-element.14.refs_0_, bf16[2048,2048]{1,0:T(8,128)(2,1)S(1)} %get-tuple-element.15.refs_1_, ...), custom_call_target="tpu_custom_call" | custom-call | tf_op jit(solution)/shard_map/pallas_call | solution.py:455

commit v7 on v6

--- a/solution.py
+++ b/solution.py
@@ -200,21 +200,23 @@
     pl.when(z > 0)(lambda: tell(2))
     for c in loads:
         c.wait()
-    pl.when(z < half)(lambda: more(0, *EARLY[::-1]))
-    pl.when((z > 0) & (z < half))(lambda: more(1, *EARLY[::-1]))
+    pl.when(z < half - 1)(lambda: more(0, *EARLY[::-1]))
+    pl.when((z > 0) & (z < half - 1))(lambda: more(1, *EARLY[::-1]))
     gain = n_in[0] + n_in[1]
     ybuf[pl.ds(col, 1)] = jnp.concatenate([gain] * ny, axis=1)[None]
     maxima(0)
+
+    low(0).start()
+    pl.when(z > 0)(lambda: low(1).start())
+    maxima(1)
 
     @pl.when(low_end)
     def _():
         pl.semaphore_wait(answer.at[1], 1)
         tell(2)
-        begin(1)
-
-    for d in range(2):
-        low(d).start()
-    maxima(1)
+        ring(1, 0).start()
+        low(1).start()
+
     know(2)
     tell(3)
     pl.when(core == 1)(lambda: pl.semaphore_wait(answer.at[2], 1))
@@ -239,10 +241,11 @@
         more(d, early + 1, own)
 
     def by_start(what):
-        pl.when(z < half)(lambda: what(0, EARLY[0]))
-        pl.when(z >= half)(lambda: what(0, EARLY[1]))
-        pl.when((z > 0) & (z < half))(lambda: what(1, EARLY[0]))
-        pl.when((z >= half) | low_end)(lambda: what(1, EARLY[1]))
+        pl.when(z < half - 1)(lambda: what(0, EARLY[0]))
+        pl.when(z >= half - 1)(lambda: what(0, EARLY[1]))
+        pl.when((z > 0) & (z < half - 1))(lambda: what(1, EARLY[0]))
+        pl.when(z >= half - 1)(lambda: what(1, EARLY[1]))
+        pl.when(low_end)(lambda: what(1, 1))
 
     by_start(gap)
     know(3)
@@ -300,6 +303,9 @@
                     low(d).wait_recv()
                 ring(d, i - own).wait_recv()
                 near(d, i - own)
+        if i == pieces - 1:
+            for via, m, here in rest_out:
+                pl.when(here)(lambda: rest_ring(via, m).start())
         for d in range(2):
             drain(d, i - DEPTH)
             ring(d, i).start()
@@ -323,8 +329,6 @@
         if i - LAG >= own:
             for d in range(2):
                 receive(d, i - LAG)
-    for via, m, here in rest_out:
-        pl.when(here)(lambda: rest_ring(via, m).start())
     norm_pair.wait_recv()
     for k in range(nz):
         for c in range(2):
@@ -347,7 +351,7 @@
     early = [(m, slot) for m in range(2) for slot in range(nz) if slot not in (half - 1, half, half + 1)]
     for m, slot in early:
         pair_got(m, slot)
-    for i in range(pieces - LAG, pieces):
+    for i in range(pieces - LAG, pieces - 1):
         for d in range(2):
             receive(d, i)
     for via, m, here in rest_in:
@@ -358,6 +362,8 @@
             rest_pair(via, m).start()
 
 
+    for d in range(2):
+        receive(d, pieces - 1)
     for slot in (half - 1, half, half + 1):
         for m in range(2):
             if (m, slot) not in early:

time: 95.4 us -> 95.4 us (level)
  no operation moved by 1% of the time
where the time goes in v7:
time: 95.4 us
  Pallas kernels  94.7 us (99%)
    pallas_call x1, Pallas kernels, per_device(): pl.pallas_call(functools.partial(kernel, nz, ny), out_shape=(pltpu.VMEM((...  88.8 us
    pallas_call x1, Pallas kernels, per_device(): pl.pallas_call(functools.partial(write_out, parts), out_shape=(jax.ShapeD...  5.96 us

profile of v7, /device:TPU:1, one launch (start us, length us, event | category | flops | bytes accessed | tf_op | source)
XLA Modules:
  0.0 95.4 jit_solution(1733342319665804117)
XLA Ops:
  0.6 88.8 %shard_map.119 = (bf16[2048,2048]{1,0:T(8,128)(2,1)S(1)}, bf16[2048,2048]{1,0:T(8,128)(2,1)S(1)}, f32[2,16,128]{2,1,0:T(8,128)S(1)}, f32[16,128]{1,0:T(8,128)S(1)}) custom-call(bf16[128,2048]{1,0:T(8,128)(2,1)} %wg_hbm.1, bf16[32,128]{1,0:T(8,128)(2,1)} %bitcast.7, bf16[32,2048]{1,0:T(8,128)(2,1)} %hg_hbm.1, bf16[128,2048]{1,0:T(8,128)(2,1)} %wu_hbm.1, ...), custom_call_target="tpu_custom_call" | custom-call | tf_op jit(solution)/shard_map/pallas_call | solution.py:409
  89.4 6.0 %shard_map.120 = (bf16[2048,2048]{1,0:T(8,128)(2,1)}, bf16[2048,2048]{1,0:T(8,128)(2,1)}, f32[16,128]{1,0:T(8,128)}, f32[16,128]{1,0:T(8,128)}, bf16[16,128]{1,0:T(8,128)(2,1)}) custom-call(bf16[2048,2048]{1,0:T(8,128)(2,1)S(1)} %get-tuple-element.14.refs_0_, bf16[2048,2048]{1,0:T(8,128)(2,1)S(1)} %get-tuple-element.15.refs_1_, ...), custom_call_target="tpu_custom_call" | custom-call | tf_op jit(solution)/shard_map/pallas_call | solution.py:461

commit v8 on v7

--- a/solution.py
+++ b/solution.py
@@ -49,8 +49,9 @@
             )
         )
     ]
-    for c in loads:
-        c.start()
+    def start_loads():
+        for c in loads:
+            c.start()
 
     barrier = pltpu.get_barrier_semaphore()
     peer = zero + 1 - 2 * core
@@ -67,6 +68,9 @@
     pl.when(low_end | high_end)(lambda: signal(barrier, "zero", to[1]))
     pl.when(core == 1)(lambda: signal(barrier, "zero", peer))
     pl.when(sides[0])(lambda: signal(barrier, "cols", beside[0]))
+
+    feeds = (z == 1) | high_end
+    pl.when(jnp.logical_not(feeds))(start_loads)
 
     def greeted():
         count = sum(c.astype(jnp.int32) for c in (z > 0, z == nz - 2, core == 0, sides[1]))
@@ -189,8 +193,10 @@
             ring(d, i).start()
 
     pl.when((z > 0) & (z < nz - 1))(lambda: begin(1))
+    pl.when(z == 1)(start_loads)
     pl.when(z < nz - 2)(lambda: pl.semaphore_wait(answer.at[0], 1))
     begin(0)
+    pl.when(high_end)(start_loads)
 
     @pl.when(high_end)
     def _():

time: 95.4 us -> 95.5 us (level)
  no operation moved by 1% of the time
where the time goes in v8:
time: 95.5 us; the launch traced here: 95.4 us
  Pallas kernels  94.7 us (99%)
    pallas_call x1, Pallas kernels, per_device(): pl.pallas_call(functools.partial(kernel, nz, ny), out_shape=(pltpu.VMEM((...  88.8 us
    pallas_call x1, Pallas kernels, per_device(): pl.pallas_call(functools.partial(write_out, parts), out_shape=(jax.ShapeD...  5.96 us

profile of v8, /device:TPU:1, one launch (start us, length us, event | category | flops | bytes accessed | tf_op | source)
XLA Modules:
  0.0 95.4 jit_solution(8543566716966022128)
XLA Ops:
  0.6 88.8 %shard_map.119 = (bf16[2048,2048]{1,0:T(8,128)(2,1)S(1)}, bf16[2048,2048]{1,0:T(8,128)(2,1)S(1)}, f32[2,16,128]{2,1,0:T(8,128)S(1)}, f32[16,128]{1,0:T(8,128)S(1)}) custom-call(bf16[128,2048]{1,0:T(8,128)(2,1)} %wg_hbm.1, bf16[32,128]{1,0:T(8,128)(2,1)} %bitcast.7, bf16[32,2048]{1,0:T(8,128)(2,1)} %hg_hbm.1, bf16[128,2048]{1,0:T(8,128)(2,1)} %wu_hbm.1, ...), custom_call_target="tpu_custom_call" | custom-call | tf_op jit(solution)/shard_map/pallas_call | solution.py:415
  89.4 6.0 %shard_map.120 = (bf16[2048,2048]{1,0:T(8,128)(2,1)}, bf16[2048,2048]{1,0:T(8,128)(2,1)}, f32[16,128]{1,0:T(8,128)}, f32[16,128]{1,0:T(8,128)}, bf16[16,128]{1,0:T(8,128)(2,1)}) custom-call(bf16[2048,2048]{1,0:T(8,128)(2,1)S(1)} %get-tuple-element.14.refs_0_, bf16[2048,2048]{1,0:T(8,128)(2,1)S(1)} %get-tuple-element.15.refs_1_, ...), custom_call_target="tpu_custom_call" | custom-call | tf_op jit(solution)/shard_map/pallas_call | solution.py:467

commit v9 on v7

--- a/solution.py
+++ b/solution.py
@@ -49,9 +49,6 @@
             )
         )
     ]
-    for c in loads:
-        c.start()
-
     barrier = pltpu.get_barrier_semaphore()
     peer = zero + 1 - 2 * core
     to = ((z + 1) % nz * 2 + core, (z + nz - 1) % nz * 2 + core)
@@ -67,6 +64,9 @@
     pl.when(low_end | high_end)(lambda: signal(barrier, "zero", to[1]))
     pl.when(core == 1)(lambda: signal(barrier, "zero", peer))
     pl.when(sides[0])(lambda: signal(barrier, "cols", beside[0]))
+
+    for c in loads:
+        c.start()
 
     def greeted():
         count = sum(c.astype(jnp.int32) for c in (z > 0, z == nz - 2, core == 0, sides[1]))

time: 95.4 us -> 95.5 us (level)
  no operation moved by 1% of the time
where the time goes in v9:
time: 95.5 us; the launch traced here: 95.4 us
  Pallas kernels  94.7 us (99%)
    pallas_call x1, Pallas kernels, per_device(): pl.pallas_call(functools.partial(kernel, nz, ny), out_shape=(pltpu.VMEM((...  88.8 us
    pallas_call x1, Pallas kernels, per_device(): pl.pallas_call(functools.partial(write_out, parts), out_shape=(jax.ShapeD...  5.96 us

profile of v9, /device:TPU:1, one launch (start us, length us, event | category | flops | bytes accessed | tf_op | source)
XLA Modules:
  0.0 95.4 jit_solution(17752098077175242644)
XLA Ops:
  0.6 88.8 %shard_map.119 = (bf16[2048,2048]{1,0:T(8,128)(2,1)S(1)}, bf16[2048,2048]{1,0:T(8,128)(2,1)S(1)}, f32[2,16,128]{2,1,0:T(8,128)S(1)}, f32[16,128]{1,0:T(8,128)S(1)}) custom-call(bf16[128,2048]{1,0:T(8,128)(2,1)} %wg_hbm.1, bf16[32,128]{1,0:T(8,128)(2,1)} %bitcast.7, bf16[32,2048]{1,0:T(8,128)(2,1)} %hg_hbm.1, bf16[128,2048]{1,0:T(8,128)(2,1)} %wu_hbm.1, ...), custom_call_target="tpu_custom_call" | custom-call | tf_op jit(solution)/shard_map/pallas_call | solution.py:409
  89.4 6.0 %shard_map.120 = (bf16[2048,2048]{1,0:T(8,128)(2,1)}, bf16[2048,2048]{1,0:T(8,128)(2,1)}, f32[16,128]{1,0:T(8,128)}, f32[16,128]{1,0:T(8,128)}, bf16[16,128]{1,0:T(8,128)(2,1)}) custom-call(bf16[2048,2048]{1,0:T(8,128)(2,1)S(1)} %get-tuple-element.14.refs_0_, bf16[2048,2048]{1,0:T(8,128)(2,1)S(1)} %get-tuple-element.15.refs_1_, ...), custom_call_target="tpu_custom_call" | custom-call | tf_op jit(solution)/shard_map/pallas_call | solution.py:461
